TPU v7x, 128 devices: a whole 4x4x4 slice. The times are simulated.
128 devices in a mesh: vocab: 64 (over x, y, z), dp: 2 (over core).
Axes of the slice: x: 4, y: 4, z: 4, core: 2. Of those that a mesh axis runs over, the one named last changes fastest.
Arguments:
- embed_table: bfloat16 [65536, 4096], P('vocab'), may hold values from -3 to 3
- token_ids: int32 [2, 65536], P('dp', 'vocab'), may hold values from 0 to 65535, as said below
- grad_rows: bfloat16 [2, 65536, 4096], P('dp', 'vocab'), may hold values from -12 to 12
Outputs:
- updated: bfloat16 [65536, 4096], P('vocab', 'dp')
- grad_rms: float32 [1], replicated
Inputs may be any that keep to these rules, and one draw needn't show every extreme that they name: `token_ids`: rows are read cyclically: row r stands for every r + k * 65536. The window of vocab index v (tokens v * 1024 to (v + 1) * 1024 - 1 of a replica) holds ids that, read as the cyclic representatives from v * 1024 - 256 to (v + 1) * 1024 + 255, rise (never fall) along its tokens; both ends are reached in some window. Only its first 128 and last 128 tokens may lie outside rows v * 1024 to (v + 1) * 1024 - 1 (so read), the first ones below, the last ones above; in every window its first token lies below and its last above, in some window all first 128 lie below, in some all last 128 above.
All inputs are finite; a program needn't handle non-finite values.
Results may differ from a plain program's by a relative error of at most 0.002.
Values may be sent and summed in bfloat16 or wider, within the bound.
No kernel may reach another device: no remote copies, remote signals or barrier semaphores. Data moves between devices by JAX's collectives and lax.ppermute only.
A program may use at most 128 MiB of HBM per device.

v0:
```python
import jax
import jax.numpy as jnp
from jax import lax
from jax.experimental import pallas as pl
from jax.experimental.pallas import tpu as pltpu
from jax.sharding import Mesh
from jax.sharding import PartitionSpec as P

VOCAB = ("vocab_0", "vocab_1", "vocab_2")
VOCAB_DP = ("vocab_0", "vocab_1", "vocab_2", "dp")
TOK_EDGE = 128
EDGE = 256
LANES = 128
TAIL = 16

step_rate = 0.5
norm_limit = 1.0


MIB = 1 << 20


def own_index():
    vocab = 0
    for name in VOCAB:
        vocab = vocab * lax.axis_size(name) + lax.axis_index(name)
    return vocab, lax.axis_index("dp")


def in_vmem(value):
    return pltpu.with_memory_space_constraint(value, pltpu.VMEM)


def in_hbm(value):
    return pltpu.with_memory_space_constraint(value, pltpu.HBM)


def any_spec():
    return pl.BlockSpec(memory_space=pltpu.HBM)


def vmem_spec():
    return pl.BlockSpec(memory_space=pltpu.VMEM)


def halves(value):
    high = lax.shift_right_logical(value, 8)
    low = jnp.bitwise_and(value, 255)
    return high.astype(jnp.float32), low.astype(jnp.float32)


def joined(high, low):
    return high.astype(jnp.int32) * 256 + low.astype(jnp.int32)


def pack(grad_rows, token_ids, rows_dev, vocab_rows, edges, swap):
    tokens, width = grad_rows.shape
    half = width // 2
    tiles = half // LANES
    depth = tiles * TOK_EDGE
    parts = 8

    def kernel(rows, ids_in, *refs):
        outs, (ids, sems) = refs[:-2], refs[-2:]
        vocab, core = own_index()
        copies = [pltpu.make_async_copy(ids_in, ids, sems.at[0])]
        for out, (at, crossed) in zip(outs, edges):
            columns = pl.multiple_of((1 - core if crossed else core) * half, half)
            for c in range(tiles):
                copies.append(
                    pltpu.make_async_copy(
                        rows.at[pl.ds(at, TOK_EDGE), pl.ds(columns + c * LANES, LANES)],
                        out.at[pl.ds(c * TOK_EDGE, TOK_EDGE), :],
                        sems.at[1],
                    )
                )
        if swap:
            columns = pl.multiple_of((1 - core) * half, half)
            step = tokens // parts
            for k in range(parts):
                copies.append(
                    pltpu.make_async_copy(
                        rows.at[pl.ds(k * step, step), pl.ds(columns, half)],
                        outs[-1].at[pl.ds(k * step, step), :],
                        sems.at[1],
                    )
                )
        for copy in copies:
            copy.start()
        copies[0].wait()
        offset = jnp.bitwise_and(ids[...] - vocab * rows_dev + EDGE, vocab_rows - 1)
        for out, (at, _) in zip(outs, edges):
            high, low = halves(offset[:, at : at + TOK_EDGE])
            upper = lax.broadcasted_iota(jnp.int32, (TAIL, LANES), 0) < TAIL // 2
            out[pl.ds(depth, TAIL), :] = jnp.where(upper, high, low).astype(out.dtype)
        if swap:
            both = jnp.concatenate(halves(offset), axis=1)
            outs[-1][pl.ds(tokens, TAIL), :] = jnp.broadcast_to(both, (TAIL, half)).astype(grad_rows.dtype)
        for copy in copies[1:]:
            copy.wait()

    shapes = [pltpu.VMEM((depth + TAIL, LANES), grad_rows.dtype)] * len(edges)
    if swap:
        shapes.append(pltpu.VMEM((tokens + TAIL, half), grad_rows.dtype))
    return pl.pallas_call(
        kernel,
        out_shape=shapes,
        in_specs=[any_spec(), any_spec()],
        out_specs=[vmem_spec()] * len(shapes),
        scratch_shapes=[pltpu.VMEM((1, tokens), jnp.int32), pltpu.SemaphoreType.DMA((2,))],
        compiler_params=pltpu.CompilerParams(vmem_limit_bytes=8 * MIB),
    )(in_hbm(grad_rows), in_hbm(token_ids))


def local_gradient(grad_rows, swapped, own_ids, embed_table, vocab_rows):
    tokens, width = grad_rows.shape
    rows_dev = embed_table.shape[0]
    half = width // 2
    block = 256
    lanes = 512

    def kernel(rows, far_rows, ids, table, grad, own_table, squares, own_rows, hot, far_hot, sems):
        vocab, core = own_index()
        own = pl.multiple_of(core * half, half)
        copies = [
            pltpu.make_async_copy(
                rows.at[:, pl.ds(own + k * lanes, lanes)], own_rows.at[:, pl.ds(k * lanes, lanes)], sems.at[k]
            )
            for k in range(half // lanes)
        ]
        for copy in copies:
            copy.start()
        table_copies = [
            pltpu.make_async_copy(
                table.at[:, pl.ds(own + k * LANES, LANES)], own_table.at[k], sems.at[half // lanes]
            )
            for k in range(half // LANES)
        ]
        for copy in table_copies:
            copy.start()
        start = vocab * rows_dev
        sent = far_rows[pl.ds(tokens, TAIL), :].astype(jnp.float32)[:1, :]
        far_local = joined(sent[:, :tokens], sent[:, tokens:]) - EDGE
        own_local = jnp.bitwise_and(ids[...] - start, vocab_rows - 1)
        for one_hot, local in ((hot, own_local), (far_hot, far_local)):
            for k in range(rows_dev // block):
                at = lax.broadcasted_iota(jnp.int32, (block, tokens), 0) + k * block
                one_hot[pl.ds(k * block, block), :] = jnp.where(at == local, 1.0, 0.0).astype(jnp.bfloat16)
        total = jnp.zeros((1, lanes), jnp.float32)
        for c in range(half // lanes):
            copies[c].wait()
            for r in range(rows_dev // block):
                part = jnp.dot(
                    hot[pl.ds(r * block, block), :],
                    own_rows[:, pl.ds(c * lanes, lanes)],
                    preferred_element_type=jnp.float32,
                ) + jnp.dot(
                    far_hot[pl.ds(r * block, block), :],
                    far_rows[pl.ds(0, tokens), pl.ds(c * lanes, lanes)],
                    preferred_element_type=jnp.float32,
                )
                grad[pl.ds(r * block, block), pl.ds(c * lanes, lanes)] = part
                if EDGE <= r * block < rows_dev - EDGE:
                    total = total + jnp.sum(part * part, axis=0, keepdims=True)
        fold = total[:, :128]
        for k in range(1, lanes // 128):
            fold = fold + total[:, k * 128 : (k + 1) * 128]
        squares[...] = fold
        for copy in table_copies:
            copy.wait()

    return pl.pallas_call(
        kernel,
        out_shape=[
            pltpu.VMEM((rows_dev, half), jnp.float32),
            pltpu.VMEM((half // LANES, rows_dev, LANES), embed_table.dtype),
            pltpu.VMEM((1, 128), jnp.float32),
        ],
        in_specs=[any_spec(), vmem_spec(), vmem_spec(), any_spec()],
        out_specs=[vmem_spec()] * 3,
        scratch_shapes=[
            pltpu.VMEM((tokens, half), grad_rows.dtype),
            pltpu.VMEM((rows_dev, tokens), jnp.bfloat16),
            pltpu.VMEM((rows_dev, tokens), jnp.bfloat16),
            pltpu.SemaphoreType.DMA((half // lanes + 1,)),
        ],
        compiler_params=pltpu.CompilerParams(vmem_limit_bytes=18 * MIB),
        cost_estimate=pl.CostEstimate(
            flops=4 * rows_dev * tokens * half, bytes_accessed=8 * MIB, transcendentals=0
        ),
        name="local_gradient",
    )(in_hbm(grad_rows), in_vmem(swapped), own_ids, in_hbm(embed_table))


def edge_gradient(grad, squares, same, cross, side, spread_rows):
    rows_dev, half = grad.shape
    group = 4
    lanes = group * LANES
    depth = half // LANES * TOK_EDGE
    base = rows_dev - EDGE if side < 0 else 0
    first = 0 if side < 0 else rows_dev + EDGE

    def kernel(grad_in, squares_in, same, cross, grad_out, spread):
        total = jnp.zeros((8, lanes), jnp.float32)
        at = lax.broadcasted_iota(jnp.int32, (EDGE, TOK_EDGE), 0) + first
        hot = []
        for part in (same, cross):
            sent = part[pl.ds(depth, TAIL), :].astype(jnp.float32)
            offset = joined(sent[:1, :], sent[TAIL // 2 : TAIL // 2 + 1, :])
            hot.append(jnp.where(at == offset, 1.0, 0.0).astype(jnp.bfloat16))
        hot = jnp.concatenate(hot, axis=1)
        for c in range(half // lanes):
            columns = pl.ds(c * lanes, lanes)
            rows = jnp.concatenate(
                [
                    jnp.concatenate(
                        [part[pl.ds((c * group + g) * TOK_EDGE, TOK_EDGE), :] for g in range(group)], axis=1
                    )
                    for part in (same, cross)
                ],
                axis=0,
            )
            value = grad_in[pl.ds(base, EDGE), columns] + jnp.dot(
                hot, rows, preferred_element_type=jnp.float32
            )
            grad_out[pl.ds(base, EDGE), columns] = value
            total = total + jnp.sum((value * value).reshape(EDGE // 8, 8, lanes), axis=0)
        total = jnp.sum(total, axis=0, keepdims=True)
        fold = squares_in[...]
        for k in range(group):
            fold = fold + total[:, k * LANES : (k + 1) * LANES]
        spread[...] = jnp.broadcast_to(fold, (spread_rows, LANES))

    return pl.pallas_call(
        kernel,
        out_shape=[
            pltpu.VMEM((rows_dev, half), jnp.float32),
            pltpu.VMEM((spread_rows, LANES), jnp.float32),
        ],
        in_specs=[vmem_spec()] * 4,
        out_specs=[vmem_spec()] * 2,
        input_output_aliases={0: 0},
        compiler_params=pltpu.CompilerParams(vmem_limit_bytes=4 * MIB),
        cost_estimate=pl.CostEstimate(flops=4 * EDGE * TOK_EDGE * half, bytes_accessed=2 * MIB, transcendentals=0),
    )(in_vmem(grad), in_vmem(squares), in_vmem(same), in_vmem(cross))


def clipped_update(grad, own_table, partials, element_count):
    rows_dev, half = grad.shape
    tiles = half // LANES
    step = 64

    def kernel(grad_in, table_in, sums, updated, rms_out, stage, rms, sems):
        total = jnp.sum(jnp.sum(sums[...], axis=0, keepdims=True), axis=1, keepdims=True)
        grad_rms = jnp.sqrt(total / element_count)
        clip_scale = 1.0 / jnp.maximum(1.0, grad_rms / norm_limit)
        rate = step_rate * clip_scale
        rms[0] = grad_rms[0, 0]
        copies = [pltpu.make_async_copy(rms, rms_out, sems.at[tiles])]
        copies[0].start()
        for c in range(tiles):
            columns = pl.ds(c * LANES, LANES)
            for r in range(0, rows_dev, step):
                rows = pl.ds(r, step)
                stage[c, rows, :] = (
                    table_in[c, rows, :].astype(jnp.float32) - rate * grad_in[rows, columns]
                ).astype(stage.dtype)
            copies.append(pltpu.make_async_copy(stage.at[c], updated.at[:, columns], sems.at[c]))
            copies[-1].start()
        for copy in copies:
            copy.wait()

    return pl.pallas_call(
        kernel,
        out_shape=[
            jax.ShapeDtypeStruct((rows_dev, half), own_table.dtype),
            jax.ShapeDtypeStruct((1,), jnp.float32),
        ],
        in_specs=[vmem_spec()] * 3,
        out_specs=[any_spec(), any_spec()],
        scratch_shapes=[
            pltpu.VMEM((tiles, rows_dev, LANES), own_table.dtype),
            pltpu.SMEM((1,), jnp.float32),
            pltpu.SemaphoreType.DMA((tiles + 1,)),
        ],
        compiler_params=pltpu.CompilerParams(vmem_limit_bytes=8 * MIB),
        name="clipped_update",
    )(in_vmem(grad), in_vmem(own_table), in_vmem(partials))


def routes(vocab_count, replicas, step, flip):
    return [
        (v * replicas + p, (v + step) % vocab_count * replicas + (1 - p if flip else p))
        for v in range(vocab_count)
        for p in range(replicas)
    ]


def body(embed_table, token_ids, grad_rows):
    rows_dev, width = embed_table.shape
    vocab_count = lax.axis_size(VOCAB)
    vocab_rows = rows_dev * vocab_count
    replicas = lax.axis_size("dp")
    devices = vocab_count * replicas
    rows = grad_rows[0]

    def sent(piece, step, flip):
        return lax.ppermute(piece, VOCAB_DP, routes(vocab_count, replicas, step, flip))

    last = token_ids.shape[1] - TOK_EDGE
    shape = (rows_dev, vocab_rows)
    plus_same, minus_same = pack(rows, token_ids, *shape, ((last, False), (0, False)), False)
    plus_same = sent(plus_same, 1, False)
    minus_same = sent(minus_same, -1, False)
    plus_cross, minus_cross, far = pack(rows, token_ids, *shape, ((last, True), (0, True)), True)
    far = sent(far, 0, True)
    plus_cross = sent(plus_cross, 1, True)
    minus_cross = sent(minus_cross, -1, True)
    grad, own_table, squares = local_gradient(rows, far, token_ids, embed_table, vocab_rows)
    grad, squares = edge_gradient(grad, squares, plus_same, plus_cross, 1, 1)
    grad, spread = edge_gradient(grad, squares, minus_same, minus_cross, -1, devices)
    partials = lax.all_to_all(spread, VOCAB_DP, 0, 0, tiled=True)
    return tuple(clipped_update(grad, own_table, partials, vocab_rows * width))


def solution(mesh):
    split = Mesh(
        mesh.devices.reshape(4, 4, 4, mesh.shape["dp"]), ("vocab_0", "vocab_1", "vocab_2", "dp")
    )
    return jax.shard_map(
        body,
        mesh=split,
        in_specs=(P(VOCAB, None), P("dp", VOCAB), P("dp", VOCAB, None)),
        out_specs=(P(VOCAB, "dp"), P()),
        check_vma=False,
    )
```

profile of v0, /device:TPU:1, one launch (start us, length us, event | category | flops | bytes accessed | tf_op | source)
XLA Modules:
  0.0 58.7 jit_solution(1251684936338815455)
XLA Ops:
  0.6 0.0 copy-start
  0.6 2.7 %shard_map.50 = (bf16[2064,128]{1,0:T(8,128)(2,1)S(1)}, bf16[2064,128]{1,0:T(8,128)(2,1)S(1)}, bf16[1040,2048]{1,0:T(8,128)(2,1)S(1)}) custom-call(bf16[1024,4096]{1,0:T(8,128)(2,1)} %bitcast.7, s32[1,1024]{1,0:T(1,128)} %ids_in.3), custom_call_target="tpu_custom_call" | custom-call | tf_op jit(solution)/shard_map/pallas_call | solution.py:105
  3.3 1.5 %collective-permute-start = (bf16[1040,2048]{1,0:T(8,128)(2,1)S(1)}, bf16[1040,2048]{1,0:T(8,128)(2,1)S(1)}, u32[]{:S(2)}, u32[]{:S(2)}) collective-permute-start(bf16[1040,2048]{1,0:T(8,128)(2,1)S(1)} %get-tuple-element.14), channel_id=1, source_target_pairs={{0,1},{1,0},{2,3},{3,2},{4,5},{5,4},{6,7},{7,6},{8,9},{9,8},{10,11... | collective-permute-start | bytes 12779528 | tf_op jit(solution)/shard_map/ppermute | solution.py:308
  4.8 1.2 %shard_map.51 = (bf16[2064,128]{1,0:T(8,128)(2,1)S(1)}, bf16[2064,128]{1,0:T(8,128)(2,1)S(1)}) custom-call(bf16[1024,4096]{1,0:T(8,128)(2,1)} %bitcast.8, s32[1,1024]{1,0:T(1,128)} %ids_in.3), custom_call_target="tpu_custom_call" | custom-call | tf_op jit(solution)/shard_map/pallas_call | solution.py:105
  6.0 1.8 %collective-permute-start.1 = (bf16[2064,128]{1,0:T(8,128)(2,1)S(1)}, bf16[2064,128]{1,0:T(8,128)(2,1)S(1)}, u32[]{:S(2)}, u32[]{:S(2)}) collective-permute-start(bf16[2064,128]{1,0:T(8,128)(2,1)S(1)} %get-tuple-element.17), channel_id=1, source_target_pairs={{0,2},{1,3},{2,4},{3,5},{4,6},{5,7},{6,8},{7,9},{8,10},{9,11},{10,... | collective-permute-start | bytes 1585160 | tf_op jit(solution)/shard_map/ppermute | solution.py:308
  7.8 6.8 %collective-permute-start.3 = (bf16[2064,128]{1,0:T(8,128)(2,1)S(1)}, bf16[2064,128]{1,0:T(8,128)(2,1)S(1)}, u32[]{:S(2)}, u32[]{:S(2)}) collective-permute-start(bf16[2064,128]{1,0:T(8,128)(2,1)S(1)} %get-tuple-element.21), channel_id=1, source_target_pairs={{0,126},{1,127},{2,0},{3,1},{4,2},{5,3},{6,4},{7,5},{8,6},{9,7},{1... | collective-permute-start | bytes 1585160 | tf_op jit(solution)/shard_map/ppermute | solution.py:308
  14.7 0.0 collective-permute-start.2
  14.7 7.2 %collective-permute-start.4 = (bf16[2064,128]{1,0:T(8,128)(2,1)S(1)}, bf16[2064,128]{1,0:T(8,128)(2,1)S(1)}, u32[]{:S(2)}, u32[]{:S(2)}) collective-permute-start(bf16[2064,128]{1,0:T(8,128)(2,1)S(1)} %get-tuple-element.22), channel_id=1, source_target_pairs={{0,127},{1,126},{2,1},{3,0},{4,3},{5,2},{6,5},{7,4},{8,7},{9,6},{1... | collective-permute-start | bytes 1585160 | tf_op jit(solution)/shard_map/ppermute | solution.py:308
  21.8 0.0 collective-permute-done.far_rows
  21.8 0.0 copy-done
  21.8 10.7 %local_gradient.1 = (f32[1024,2048]{1,0:T(8,128)S(1)}, bf16[16,1024,128]{2,1,0:T(8,128)(2,1)S(1)}, f32[1,128]{1,0:T(1,128)S(1)}) custom-call(bf16[1024,4096]{1,0:T(8,128)(2,1)} %bitcast.9, bf16[1040,2048]{1,0:T(8,128)(2,1)S(1)} %collective-permute-done.far_rows, s32[1,1024]{1,0:T(1,128)S(1)} %copy-done, bf16[1024,4096]{1,0:T(8,128)(2,1)} %table.1), custom_call_target="tpu_custom_call" | custom-call | flops 8589934592 | bytes 8388608 | tf_op jit(solution)/shard_map/local_gradient/pallas_call | solution.py:172
  32.5 0.0 collective-permute-done.1.same
  32.5 5.7 %collective-permute-done.2.cross = bf16[2064,128]{1,0:T(8,128)(2,1)S(1)} collective-permute-done((bf16[2064,128]{1,0:T(8,128)(2,1)S(1)}, bf16[2064,128]{1,0:T(8,128)(2,1)S(1)}, u32[]{:S(2)}, u32[]{:S(2)}) %collective-permute-start.2) | collective-permute-done | bytes 528416 | tf_op jit(solution)/shard_map/ppermute | solution.py:308
  38.3 0.7 %shard_map.52 = (f32[1024,2048]{1,0:T(8,128)S(1)}, f32[1,128]{1,0:T(1,128)S(1)}) custom-call(f32[1024,2048]{1,0:T(8,128)S(1)} %get-tuple-element.15.grad_in, f32[1,128]{1,0:T(1,128)S(1)} %get-tuple-element.16.squares_in, bf16[2064,128]{1,0:T(8,128)(2,1)S(1)} %collective-permute-done.1.same, ...), custom_call_target="tpu_custom_call", output_to_operand_aliasing={{0}: (0, {})} | custom-call | flops 268435456 | bytes 2097152 | tf_op jit(solution)/shard_map/pallas_call | solution.py:234
  39.0 0.0 collective-permute-done.3.same
  39.0 0.0 collective-permute-done.4.cross
  39.0 0.7 %shard_map.53 = (f32[1024,2048]{1,0:T(8,128)S(1)}, f32[128,128]{1,0:T(8,128)S(1)}) custom-call(f32[1024,2048]{1,0:T(8,128)S(1)} %get-tuple-element.19.grad_in, f32[1,128]{1,0:T(1,128)S(1)} %get-tuple-element.20.squares_in, bf16[2064,128]{1,0:T(8,128)(2,1)S(1)} %collective-permute-done.3.same, ...), custom_call_target="tpu_custom_call", output_to_operand_aliasing={{0}: (0, {})} | custom-call | flops 268435456 | bytes 2097152 | tf_op jit(solution)/shard_map/pallas_call | solution.py:234
  39.7 16.7 %all_to_all.11 = f32[128,1,128]{2,1,0:T(1,128)S(1)} all-to-all(f32[128,1,128]{2,1,0:T(1,128)S(1)} %bitcast.6), channel_id=1, replica_groups=mesh['vocab_0'=4,'vocab_1'=4,'vocab_2'=4,'dp'=2] {'vocab_0','vocab_1','v..., dimensions={0} | all-to-all | bytes 131072 | tf_op jit(solution)/shard_map/all_to_all | solution.py:322
  56.4 2.3 %clipped_update.1 = (bf16[1024,2048]{1,0:T(8,128)(2,1)}, f32[1]{0:T(128)}) custom-call(f32[1024,2048]{1,0:T(8,128)S(1)} %get-tuple-element.23.grad_in, bf16[16,1024,128]{2,1,0:T(8,128)(2,1)S(1)} %get-tuple-element.24.table_in, f32[128,128]{1,0:T(8,128)S(1)} %bitcast.5), custom_call_target="tpu_custom_call" | custom-call | tf_op jit(solution)/shard_map/clipped_update/pallas_call | solution.py:273
Async XLA Ops:
  0.6 21.2 %copy-start = (s32[1,1024]{1,0:T(1,128)S(1)}, s32[1,1024]{1,0:T(1,128)}, u32[]{:S(2)}) copy-start(s32[1,1024]{1,0:T(1,128)} %ids_in.3) | copy-start | bytes 12292
  3.3 18.5 %collective-permute-start = (bf16[1040,2048]{1,0:T(8,128)(2,1)S(1)}, bf16[1040,2048]{1,0:T(8,128)(2,1)S(1)}, u32[]{:S(2)}, u32[]{:S(2)}) collective-permute-start(bf16[1040,2048]{1,0:T(8,128)(2,1)S(1)} %get-tuple-element.14), channel_id=1, source_target_pairs={{0,1},{1,0},{2,3},{3,2},{4,5},{5,4},{6,7},{7,6},{8,9},{9,8},{10,11... | collective-permute-start | bytes 12779528 | tf_op jit(solution)/shard_map/ppermute | solution.py:308
  6.0 26.6 %collective-permute-start.1 = (bf16[2064,128]{1,0:T(8,128)(2,1)S(1)}, bf16[2064,128]{1,0:T(8,128)(2,1)S(1)}, u32[]{:S(2)}, u32[]{:S(2)}) collective-permute-start(bf16[2064,128]{1,0:T(8,128)(2,1)S(1)} %get-tuple-element.17), channel_id=1, source_target_pairs={{0,2},{1,3},{2,4},{3,5},{4,6},{5,7},{6,8},{7,9},{8,10},{9,11},{10,... | collective-permute-start | bytes 1585160 | tf_op jit(solution)/shard_map/ppermute | solution.py:308
  7.8 31.2 %collective-permute-start.3 = (bf16[2064,128]{1,0:T(8,128)(2,1)S(1)}, bf16[2064,128]{1,0:T(8,128)(2,1)S(1)}, u32[]{:S(2)}, u32[]{:S(2)}) collective-permute-start(bf16[2064,128]{1,0:T(8,128)(2,1)S(1)} %get-tuple-element.21), channel_id=1, source_target_pairs={{0,126},{1,127},{2,0},{3,1},{4,2},{5,3},{6,4},{7,5},{8,6},{9,7},{1... | collective-permute-start | bytes 1585160 | tf_op jit(solution)/shard_map/ppermute | solution.py:308
  14.7 23.6 %collective-permute-start.2 = (bf16[2064,128]{1,0:T(8,128)(2,1)S(1)}, bf16[2064,128]{1,0:T(8,128)(2,1)S(1)}, u32[]{:S(2)}, u32[]{:S(2)}) collective-permute-start(bf16[2064,128]{1,0:T(8,128)(2,1)S(1)} %get-tuple-element.18), channel_id=1, source_target_pairs={{0,3},{1,2},{2,5},{3,4},{4,7},{5,6},{6,9},{7,8},{8,11},{9,10},{10,... | collective-permute-start | bytes 1585160 | tf_op jit(solution)/shard_map/ppermute | solution.py:308
  14.7 24.3 %collective-permute-start.4 = (bf16[2064,128]{1,0:T(8,128)(2,1)S(1)}, bf16[2064,128]{1,0:T(8,128)(2,1)S(1)}, u32[]{:S(2)}, u32[]{:S(2)}) collective-permute-start(bf16[2064,128]{1,0:T(8,128)(2,1)S(1)} %get-tuple-element.22), channel_id=1, source_target_pairs={{0,127},{1,126},{2,1},{3,0},{4,3},{5,2},{6,5},{7,4},{8,7},{9,6},{1... | collective-permute-start | bytes 1585160 | tf_op jit(solution)/shard_map/ppermute | solution.py:308
where the time goes:
time: 59 us; the launch traced here: 58.7 us
  Pallas kernels  18.3 us (31%)
  starting transfers between devices  17.3 us (29%)
  blocking collectives  16.7 us (28%)
  waiting for transfers between devices  5.72 us (10%)
  between operations  0.7 us (1%)
    ppermute x5, starting transfers between devices, sent(): lax.ppermute(piece, VOCAB_DP, routes(vocab_count, replicas, step, flip))  17.3 us
    all_to_all x1, blocking collectives, body(): partials = lax.all_to_all(spread, VOCAB_DP, 0, 0, tiled=True)  16.7 us
    pallas_call x1, Pallas kernels, local_gradient(): pl.pallas_call(kernel, out_shape=[pltpu.VMEM((rows_dev, half), jnp.float3...  10.7 us
    ppermute x5, waiting for transfers between devices, sent(): lax.ppermute(piece, VOCAB_DP, routes(vocab_count, replicas, step, flip))  5.72 us
    pallas_call x2, Pallas kernels, pack(): pl.pallas_call(kernel, out_shape=shapes, in_specs=[any_spec(), any_spec()...  3.87 us
    pallas_call x1, Pallas kernels, clipped_update(): pl.pallas_call(kernel, out_shape=[jax.ShapeDtypeStruct((rows_dev, half),...  2.34 us
    pallas_call x2, Pallas kernels, edge_gradient(): pl.pallas_call(kernel, out_shape=[pltpu.VMEM((rows_dev, half), jnp.float3...  1.41 us
  transfers between devices with their start and end apart: 5, of which 1 were waited for; matrix products, arithmetic and copies ran while one was open for 0% of the time, Pallas kernels for 21%

commit v1 on v0

--- a/solution.py
+++ b/solution.py
@@ -56,20 +56,18 @@
 def pack(grad_rows, token_ids, rows_dev, vocab_rows, edges, swap):
     tokens, width = grad_rows.shape
     half = width // 2
-    tiles = half // LANES
-    depth = tiles * TOK_EDGE
     parts = 8
 
     def kernel(rows, ids_in, *refs):
         outs, (ids, sems) = refs[:-2], refs[-2:]
         vocab, core = own_index()
         copies = [pltpu.make_async_copy(ids_in, ids, sems.at[0])]
-        for out, (at, crossed) in zip(outs, edges):
+        for out, (at, crossed, first, count, _) in zip(outs, edges):
             columns = pl.multiple_of((1 - core if crossed else core) * half, half)
-            for c in range(tiles):
+            for c in range(count):
                 copies.append(
                     pltpu.make_async_copy(
-                        rows.at[pl.ds(at, TOK_EDGE), pl.ds(columns + c * LANES, LANES)],
+                        rows.at[pl.ds(at, TOK_EDGE), pl.ds(columns + (first + c) * LANES, LANES)],
                         out.at[pl.ds(c * TOK_EDGE, TOK_EDGE), :],
                         sems.at[1],
                     )
@@ -89,17 +87,21 @@
             copy.start()
         copies[0].wait()
         offset = jnp.bitwise_and(ids[...] - vocab * rows_dev + EDGE, vocab_rows - 1)
-        for out, (at, _) in zip(outs, edges):
-            high, low = halves(offset[:, at : at + TOK_EDGE])
-            upper = lax.broadcasted_iota(jnp.int32, (TAIL, LANES), 0) < TAIL // 2
-            out[pl.ds(depth, TAIL), :] = jnp.where(upper, high, low).astype(out.dtype)
+        for out, (at, _, _, count, tail) in zip(outs, edges):
+            if tail:
+                high, low = halves(offset[:, at : at + TOK_EDGE])
+                upper = lax.broadcasted_iota(jnp.int32, (TAIL, LANES), 0) < TAIL // 2
+                out[pl.ds(count * TOK_EDGE, TAIL), :] = jnp.where(upper, high, low).astype(out.dtype)
         if swap:
             both = jnp.concatenate(halves(offset), axis=1)
             outs[-1][pl.ds(tokens, TAIL), :] = jnp.broadcast_to(both, (TAIL, half)).astype(grad_rows.dtype)
         for copy in copies[1:]:
             copy.wait()
 
-    shapes = [pltpu.VMEM((depth + TAIL, LANES), grad_rows.dtype)] * len(edges)
+    shapes = [
+        pltpu.VMEM((count * TOK_EDGE + (TAIL if tail else 0), LANES), grad_rows.dtype)
+        for _, _, _, count, tail in edges
+    ]
     if swap:
         shapes.append(pltpu.VMEM((tokens + TAIL, half), grad_rows.dtype))
     return pl.pallas_call(
@@ -192,20 +194,28 @@
     )(in_hbm(grad_rows), in_vmem(swapped), own_ids, in_hbm(embed_table))
 
 
-def edge_gradient(grad, squares, same, cross, side, spread_rows):
+def edge_gradient(grad, squares, same, cross, rest, side, spread_rows):
     rows_dev, half = grad.shape
     group = 4
     lanes = group * LANES
-    depth = half // LANES * TOK_EDGE
     base = rows_dev - EDGE if side < 0 else 0
     first = 0 if side < 0 else rows_dev + EDGE
 
-    def kernel(grad_in, squares_in, same, cross, grad_out, spread):
+    def kernel(grad_in, squares_in, same, cross, *refs):
+        others, (grad_out, spread) = refs[:-2], refs[-2:]
+
+        def tile(part, k):
+            whole = part.shape[0] // TOK_EDGE
+            if k < whole:
+                return part[pl.ds(k * TOK_EDGE, TOK_EDGE), :]
+            rows = pl.ds((k - whole) * TOK_EDGE, TOK_EDGE)
+            return others[0][rows, :] + others[1][rows, :]
+
         total = jnp.zeros((8, lanes), jnp.float32)
         at = lax.broadcasted_iota(jnp.int32, (EDGE, TOK_EDGE), 0) + first
         hot = []
         for part in (same, cross):
-            sent = part[pl.ds(depth, TAIL), :].astype(jnp.float32)
+            sent = part[pl.ds(part.shape[0] - TAIL, TAIL), :].astype(jnp.float32)
             offset = joined(sent[:1, :], sent[TAIL // 2 : TAIL // 2 + 1, :])
             hot.append(jnp.where(at == offset, 1.0, 0.0).astype(jnp.bfloat16))
         hot = jnp.concatenate(hot, axis=1)
@@ -214,7 +224,7 @@
             rows = jnp.concatenate(
                 [
                     jnp.concatenate(
-                        [part[pl.ds((c * group + g) * TOK_EDGE, TOK_EDGE), :] for g in range(group)], axis=1
+                        [tile(part, c * group + g) for g in range(group)], axis=1
                     )
                     for part in (same, cross)
                 ],
@@ -237,12 +247,12 @@
             pltpu.VMEM((rows_dev, half), jnp.float32),
             pltpu.VMEM((spread_rows, LANES), jnp.float32),
         ],
-        in_specs=[vmem_spec()] * 4,
+        in_specs=[vmem_spec()] * (4 + len(rest)),
         out_specs=[vmem_spec()] * 2,
         input_output_aliases={0: 0},
         compiler_params=pltpu.CompilerParams(vmem_limit_bytes=4 * MIB),
         cost_estimate=pl.CostEstimate(flops=4 * EDGE * TOK_EDGE * half, bytes_accessed=2 * MIB, transcendentals=0),
-    )(in_vmem(grad), in_vmem(squares), in_vmem(same), in_vmem(cross))
+    )(in_vmem(grad), in_vmem(squares), in_vmem(same), in_vmem(cross), *[in_vmem(part) for part in rest])
 
 
 def clipped_update(grad, own_table, partials, element_count):
@@ -288,11 +298,12 @@
     )(in_vmem(grad), in_vmem(own_table), in_vmem(partials))
 
 
-def routes(vocab_count, replicas, step, flip):
+def routes(vocab_count, replicas, step, flip, left_out=()):
     return [
         (v * replicas + p, (v + step) % vocab_count * replicas + (1 - p if flip else p))
         for v in range(vocab_count)
         for p in range(replicas)
+        if v not in left_out
     ]
 
 
@@ -303,22 +314,50 @@
     replicas = lax.axis_size("dp")
     devices = vocab_count * replicas
     rows = grad_rows[0]
-
-    def sent(piece, step, flip):
-        return lax.ppermute(piece, VOCAB_DP, routes(vocab_count, replicas, step, flip))
+    plane = vocab_count // lax.axis_size(VOCAB[0])
+    line = lax.axis_size(VOCAB[2])
+    corners = range(0, vocab_count, plane)
+    relays = {v: v + 2 * line - 1 for v in corners}
+    to_relay = [(v * replicas + p, relays[v] * replicas + 1 - p) for v in corners for p in range(replicas)]
+    from_relay = [
+        (relays[v] * replicas + p, (v - 1) % vocab_count * replicas + p) for v in corners for p in range(replicas)
+    ]
+
+    def moved(piece, pairs):
+        return lax.ppermute(piece, VOCAB_DP, pairs)
+
+    def sent(piece, step, flip, left_out=()):
+        return moved(piece, routes(vocab_count, replicas, step, flip, left_out))
 
     last = token_ids.shape[1] - TOK_EDGE
+    tiles = width // replicas // LANES
+    kept = tiles - tiles // 4
     shape = (rows_dev, vocab_rows)
-    plus_same, minus_same = pack(rows, token_ids, *shape, ((last, False), (0, False)), False)
+    plus_same, minus_same, minus_rest = pack(
+        rows,
+        token_ids,
+        *shape,
+        (
+            (last, False, 0, tiles, True),
+            (0, False, 0, tiles, True),
+            (0, True, kept, tiles - kept, False),
+        ),
+        False,
+    )
     plus_same = sent(plus_same, 1, False)
     minus_same = sent(minus_same, -1, False)
-    plus_cross, minus_cross, far = pack(rows, token_ids, *shape, ((last, True), (0, True)), True)
+    relayed = moved(minus_rest, to_relay)
+    plus_cross, minus_cross, far = pack(
+        rows, token_ids, *shape, ((last, True, 0, tiles, True), (0, True, 0, kept, True)), True
+    )
     far = sent(far, 0, True)
+    minus_cross = sent(minus_cross, -1, True)
     plus_cross = sent(plus_cross, 1, True)
-    minus_cross = sent(minus_cross, -1, True)
+    minus_rest = sent(minus_rest, -1, True, corners)
+    relayed = moved(relayed, from_relay)
     grad, own_table, squares = local_gradient(rows, far, token_ids, embed_table, vocab_rows)
-    grad, squares = edge_gradient(grad, squares, plus_same, plus_cross, 1, 1)
-    grad, spread = edge_gradient(grad, squares, minus_same, minus_cross, -1, devices)
+    grad, squares = edge_gradient(grad, squares, plus_same, plus_cross, (), 1, 1)
+    grad, spread = edge_gradient(grad, squares, minus_same, minus_cross, (minus_rest, relayed), -1, devices)
     partials = lax.all_to_all(spread, VOCAB_DP, 0, 0, tiled=True)
     return tuple(clipped_update(grad, own_table, partials, vocab_rows * width))
 

time: 59 us -> 63.7 us (1.080)
  starting transfers between devices: 17.3 us -> 19.5 us
  blocking collectives: 16.7 us -> 18.6 us
    ppermute x5 -> x8, starting transfers between devices: 17.3 us -> 19.5 us  [moved(): return lax.ppermute(piece, VOCAB_DP, pairs)]
    all_to_all x1, blocking collectives: 16.7 us -> 18.6 us  [body(): partials = lax.all_to_all(spread, VOCAB_DP, 0, 0, tiled=True)]
    ppermute x5 -> x8, waiting for transfers between devices: 5.72 us -> 6.22 us  [moved(): return lax.ppermute(piece, VOCAB_DP, pairs)]
  transfers between devices with their start and end apart: 5 -> 8, of which waited for: 1 -> 2; matrix products, arithmetic and copies ran while one was open for 0% -> 0% of each run, Pallas kernels for 21% -> 20%
where the time goes in v1:
time: 63.7 us; the launch traced here: 63.4 us
  starting transfers between devices  19.5 us (31%)
  blocking collectives  18.6 us (29%)
  Pallas kernels  18.4 us (29%)
  waiting for transfers between devices  6.22 us (10%)
  between operations  0.74 us (1%)
    ppermute x8, starting transfers between devices, moved(): return lax.ppermute(piece, VOCAB_DP, pairs)  19.5 us
    all_to_all x1, blocking collectives, body(): partials = lax.all_to_all(spread, VOCAB_DP, 0, 0, tiled=True)  18.6 us
    pallas_call x1, Pallas kernels, local_gradient(): pl.pallas_call(kernel, out_shape=[pltpu.VMEM((rows_dev, half), jnp.float3...  10.7 us
    ppermute x8, waiting for transfers between devices, moved(): return lax.ppermute(piece, VOCAB_DP, pairs)  6.22 us
    pallas_call x2, Pallas kernels, pack(): pl.pallas_call(kernel, out_shape=shapes, in_specs=[any_spec(), any_spec()...  3.87 us
    pallas_call x1, Pallas kernels, clipped_update(): pl.pallas_call(kernel, out_shape=[jax.ShapeDtypeStruct((rows_dev, half),...  2.34 us
    pallas_call x2, Pallas kernels, edge_gradient(): pl.pallas_call(kernel, out_shape=[pltpu.VMEM((rows_dev, half), jnp.float3...  1.47 us
  transfers between devices with their start and end apart: 8, of which 2 were waited for; matrix products, arithmetic and copies ran while one was open for 0% of the time, Pallas kernels for 20%

profile of v1, /device:TPU:1, one launch (start us, length us, event | category | flops | bytes accessed | tf_op | source)
XLA Modules:
  0.0 63.4 jit_solution(321592979777475409)
XLA Ops:
  0.6 0.0 copy-start
  0.6 2.6 %shard_map.50 = (bf16[2064,128]{1,0:T(8,128)(2,1)S(1)}, bf16[1552,128]{1,0:T(8,128)(2,1)S(1)}, bf16[1040,2048]{1,0:T(8,128)(2,1)S(1)}) custom-call(bf16[1024,4096]{1,0:T(8,128)(2,1)} %bitcast.7, s32[1,1024]{1,0:T(1,128)} %ids_in.3), custom_call_target="tpu_custom_call" | custom-call | tf_op jit(solution)/shard_map/pallas_call | solution.py:107
  3.3 1.5 %collective-permute-start = (bf16[1040,2048]{1,0:T(8,128)(2,1)S(1)}, bf16[1040,2048]{1,0:T(8,128)(2,1)S(1)}, u32[]{:S(2)}, u32[]{:S(2)}) collective-permute-start(bf16[1040,2048]{1,0:T(8,128)(2,1)S(1)} %get-tuple-element.15), channel_id=1, source_target_pairs={{0,1},{1,0},{2,3},{3,2},{4,5},{5,4},{6,7},{7,6},{8,9},{9,8},{10,11... | collective-permute-start | bytes 12779528 | tf_op jit(solution)/shard_map/ppermute | solution.py:327
  4.7 1.7 %collective-permute-start.2 = (bf16[2064,128]{1,0:T(8,128)(2,1)S(1)}, bf16[2064,128]{1,0:T(8,128)(2,1)S(1)}, u32[]{:S(2)}, u32[]{:S(2)}) collective-permute-start(bf16[2064,128]{1,0:T(8,128)(2,1)S(1)} %get-tuple-element.19), channel_id=1, source_target_pairs={{0,3},{1,2},{2,5},{3,4},{4,7},{5,6},{6,9},{7,8},{8,11},{9,10},{10,... | collective-permute-start | bytes 1585160 | tf_op jit(solution)/shard_map/ppermute | solution.py:327
  6.4 1.3 %shard_map.51 = (bf16[2064,128]{1,0:T(8,128)(2,1)S(1)}, bf16[2064,128]{1,0:T(8,128)(2,1)S(1)}, bf16[512,128]{1,0:T(8,128)(2,1)S(1)}) custom-call(bf16[1024,4096]{1,0:T(8,128)(2,1)} %bitcast.8, s32[1,1024]{1,0:T(1,128)} %ids_in.3), custom_call_target="tpu_custom_call" | custom-call | tf_op jit(solution)/shard_map/pallas_call | solution.py:107
  7.7 5.3 %collective-permute-start.6 = (bf16[512,128]{1,0:T(8,128)(2,1)S(1)}, bf16[512,128]{1,0:T(8,128)(2,1)S(1)}, u32[]{:S(2)}, u32[]{:S(2)}) collective-permute-start(bf16[512,128]{1,0:T(8,128)(2,1)S(1)} %get-tuple-element.24), channel_id=1, source_target_pairs={{0,15},{1,14},{32,47},{33,46},{64,79},{65,78},{96,111},{97,110}} | collective-permute-start | bytes 393224 | tf_op jit(solution)/shard_map/ppermute | solution.py:327
  13.0 1.3 %collective-permute-start.5 = (bf16[512,128]{1,0:T(8,128)(2,1)S(1)}, bf16[512,128]{1,0:T(8,128)(2,1)S(1)}, u32[]{:S(2)}, u32[]{:S(2)}) collective-permute-start(bf16[512,128]{1,0:T(8,128)(2,1)S(1)} %get-tuple-element.24), channel_id=1, source_target_pairs={{2,1},{3,0},{4,3},{5,2},{6,5},{7,4},{8,7},{9,6},{10,9},{11,8},{12,... | collective-permute-start | bytes 393224 | tf_op jit(solution)/shard_map/ppermute | solution.py:327
  14.3 2.2 %collective-permute-start.1 = (bf16[2064,128]{1,0:T(8,128)(2,1)S(1)}, bf16[2064,128]{1,0:T(8,128)(2,1)S(1)}, u32[]{:S(2)}, u32[]{:S(2)}) collective-permute-start(bf16[2064,128]{1,0:T(8,128)(2,1)S(1)} %get-tuple-element.18), channel_id=1, source_target_pairs={{0,2},{1,3},{2,4},{3,5},{4,6},{5,7},{6,8},{7,9},{8,10},{9,11},{10,... | collective-permute-start | bytes 1585160 | tf_op jit(solution)/shard_map/ppermute | solution.py:327
  16.5 0.0 collective-permute-done.6
  16.5 5.1 %collective-permute-start.4 = (bf16[1552,128]{1,0:T(8,128)(2,1)S(1)}, bf16[1552,128]{1,0:T(8,128)(2,1)S(1)}, u32[]{:S(2)}, u32[]{:S(2)}) collective-permute-start(bf16[1552,128]{1,0:T(8,128)(2,1)S(1)} %get-tuple-element.23), channel_id=1, source_target_pairs={{0,127},{1,126},{2,1},{3,0},{4,3},{5,2},{6,5},{7,4},{8,7},{9,6},{1... | collective-permute-start | bytes 1191944 | tf_op jit(solution)/shard_map/ppermute | solution.py:327
  21.6 4.2 %collective-permute-done.2.cross = bf16[2064,128]{1,0:T(8,128)(2,1)S(1)} collective-permute-done((bf16[2064,128]{1,0:T(8,128)(2,1)S(1)}, bf16[2064,128]{1,0:T(8,128)(2,1)S(1)}, u32[]{:S(2)}, u32[]{:S(2)}) %collective-permute-start.2) | collective-permute-done | bytes 528416 | tf_op jit(solution)/shard_map/ppermute | solution.py:327
  25.8 1.8 %collective-permute-start.3 = (bf16[2064,128]{1,0:T(8,128)(2,1)S(1)}, bf16[2064,128]{1,0:T(8,128)(2,1)S(1)}, u32[]{:S(2)}, u32[]{:S(2)}) collective-permute-start(bf16[2064,128]{1,0:T(8,128)(2,1)S(1)} %get-tuple-element.22), channel_id=1, source_target_pairs={{0,126},{1,127},{2,0},{3,1},{4,2},{5,3},{6,4},{7,5},{8,6},{9,7},{1... | collective-permute-start | bytes 1585160 | tf_op jit(solution)/shard_map/ppermute | solution.py:327
  27.5 0.0 collective-permute-done.far_rows
  27.6 0.7 %collective-permute-start.7 = (bf16[512,128]{1,0:T(8,128)(2,1)S(1)}, bf16[512,128]{1,0:T(8,128)(2,1)S(1)}, u32[]{:S(2)}, u32[]{:S(2)}) collective-permute-start(bf16[512,128]{1,0:T(8,128)(2,1)S(1)} %collective-permute-done.6), channel_id=1, source_target_pairs={{14,126},{15,127},{46,30},{47,31},{78,62},{79,63},{110,94},{111,95}} | collective-permute-start | bytes 393224 | tf_op jit(solution)/shard_map/ppermute | solution.py:327
  28.2 0.0 copy-done
  28.2 10.7 %local_gradient.1 = (f32[1024,2048]{1,0:T(8,128)S(1)}, bf16[16,1024,128]{2,1,0:T(8,128)(2,1)S(1)}, f32[1,128]{1,0:T(1,128)S(1)}) custom-call(bf16[1024,4096]{1,0:T(8,128)(2,1)} %bitcast.9, bf16[1040,2048]{1,0:T(8,128)(2,1)S(1)} %collective-permute-done.far_rows, s32[1,1024]{1,0:T(1,128)S(1)} %copy-done, bf16[1024,4096]{1,0:T(8,128)(2,1)} %table.1), custom_call_target="tpu_custom_call" | custom-call | flops 8589934592 | bytes 8388608 | tf_op jit(solution)/shard_map/local_gradient/pallas_call | solution.py:174
  38.9 0.0 collective-permute-done.1.same
  38.9 0.7 %shard_map.52 = (f32[1024,2048]{1,0:T(8,128)S(1)}, f32[1,128]{1,0:T(1,128)S(1)}) custom-call(f32[1024,2048]{1,0:T(8,128)S(1)} %get-tuple-element.16.grad_in, f32[1,128]{1,0:T(1,128)S(1)} %get-tuple-element.17.squares_in, bf16[2064,128]{1,0:T(8,128)(2,1)S(1)} %collective-permute-done.1.same, ...), custom_call_target="tpu_custom_call", output_to_operand_aliasing={{0}: (0, {})} | custom-call | flops 268435456 | bytes 2097152 | tf_op jit(solution)/shard_map/pallas_call | solution.py:244
  39.7 0.0 collective-permute-done.5.refs_0_
  39.7 0.0 collective-permute-done.7.refs_1_
  39.7 0.0 collective-permute-done.4.cross
  39.7 2.1 %collective-permute-done.3.same = bf16[2064,128]{1,0:T(8,128)(2,1)S(1)} collective-permute-done((bf16[2064,128]{1,0:T(8,128)(2,1)S(1)}, bf16[2064,128]{1,0:T(8,128)(2,1)S(1)}, u32[]{:S(2)}, u32[]{:S(2)}) %collective-permute-start.3) | collective-permute-done | bytes 528416 | tf_op jit(solution)/shard_map/ppermute | solution.py:327
  41.7 0.8 %shard_map.53 = (f32[1024,2048]{1,0:T(8,128)S(1)}, f32[128,128]{1,0:T(8,128)S(1)}) custom-call(f32[1024,2048]{1,0:T(8,128)S(1)} %get-tuple-element.20.grad_in, f32[1,128]{1,0:T(1,128)S(1)} %get-tuple-element.21.squares_in, bf16[2064,128]{1,0:T(8,128)(2,1)S(1)} %collective-permute-done.3.same, ...), custom_call_target="tpu_custom_call", output_to_operand_aliasing={{0}: (0, {})} | custom-call | flops 268435456 | bytes 2097152 | tf_op jit(solution)/shard_map/pallas_call | solution.py:244
  42.5 18.6 %all_to_all.11 = f32[128,1,128]{2,1,0:T(1,128)S(1)} all-to-all(f32[128,1,128]{2,1,0:T(1,128)S(1)} %bitcast.6), channel_id=1, replica_groups=mesh['vocab_0'=4,'vocab_1'=4,'vocab_2'=4,'dp'=2] {'vocab_0','vocab_1','v..., dimensions={0} | all-to-all | bytes 131072 | tf_op jit(solution)/shard_map/all_to_all | solution.py:361
  61.1 2.3 %clipped_update.1 = (bf16[1024,2048]{1,0:T(8,128)(2,1)}, f32[1]{0:T(128)}) custom-call(f32[1024,2048]{1,0:T(8,128)S(1)} %get-tuple-element.25.grad_in, bf16[16,1024,128]{2,1,0:T(8,128)(2,1)S(1)} %get-tuple-element.26.table_in, f32[128,128]{1,0:T(8,128)S(1)} %bitcast.5), custom_call_target="tpu_custom_call" | custom-call | tf_op jit(solution)/shard_map/clipped_update/pallas_call | solution.py:283
Async XLA Ops:
  0.6 27.6 %copy-start = (s32[1,1024]{1,0:T(1,128)S(1)}, s32[1,1024]{1,0:T(1,128)}, u32[]{:S(2)}) copy-start(s32[1,1024]{1,0:T(1,128)} %ids_in.3) | copy-start | bytes 12292
  3.3 24.3 %collective-permute-start = (bf16[1040,2048]{1,0:T(8,128)(2,1)S(1)}, bf16[1040,2048]{1,0:T(8,128)(2,1)S(1)}, u32[]{:S(2)}, u32[]{:S(2)}) collective-permute-start(bf16[1040,2048]{1,0:T(8,128)(2,1)S(1)} %get-tuple-element.15), channel_id=1, source_target_pairs={{0,1},{1,0},{2,3},{3,2},{4,5},{5,4},{6,7},{7,6},{8,9},{9,8},{10,11... | collective-permute-start | bytes 12779528 | tf_op jit(solution)/shard_map/ppermute | solution.py:327
  4.7 21.1 %collective-permute-start.2 = (bf16[2064,128]{1,0:T(8,128)(2,1)S(1)}, bf16[2064,128]{1,0:T(8,128)(2,1)S(1)}, u32[]{:S(2)}, u32[]{:S(2)}) collective-permute-start(bf16[2064,128]{1,0:T(8,128)(2,1)S(1)} %get-tuple-element.19), channel_id=1, source_target_pairs={{0,3},{1,2},{2,5},{3,4},{4,7},{5,6},{6,9},{7,8},{8,11},{9,10},{10,... | collective-permute-start | bytes 1585160 | tf_op jit(solution)/shard_map/ppermute | solution.py:327
  7.7 8.8 %collective-permute-start.6 = (bf16[512,128]{1,0:T(8,128)(2,1)S(1)}, bf16[512,128]{1,0:T(8,128)(2,1)S(1)}, u32[]{:S(2)}, u32[]{:S(2)}) collective-permute-start(bf16[512,128]{1,0:T(8,128)(2,1)S(1)} %get-tuple-element.24), channel_id=1, source_target_pairs={{0,15},{1,14},{32,47},{33,46},{64,79},{65,78},{96,111},{97,110}} | collective-permute-start | bytes 393224 | tf_op jit(solution)/shard_map/ppermute | solution.py:327
  13.0 26.7 %collective-permute-start.5 = (bf16[512,128]{1,0:T(8,128)(2,1)S(1)}, bf16[512,128]{1,0:T(8,128)(2,1)S(1)}, u32[]{:S(2)}, u32[]{:S(2)}) collective-permute-start(bf16[512,128]{1,0:T(8,128)(2,1)S(1)} %get-tuple-element.24), channel_id=1, source_target_pairs={{2,1},{3,0},{4,3},{5,2},{6,5},{7,4},{8,7},{9,6},{10,9},{11,8},{12,... | collective-permute-start | bytes 393224 | tf_op jit(solution)/shard_map/ppermute | solution.py:327
  14.3 24.6 %collective-permute-start.1 = (bf16[2064,128]{1,0:T(8,128)(2,1)S(1)}, bf16[2064,128]{1,0:T(8,128)(2,1)S(1)}, u32[]{:S(2)}, u32[]{:S(2)}) collective-permute-start(bf16[2064,128]{1,0:T(8,128)(2,1)S(1)} %get-tuple-element.18), channel_id=1, source_target_pairs={{0,2},{1,3},{2,4},{3,5},{4,6},{5,7},{6,8},{7,9},{8,10},{9,11},{10,... | collective-permute-start | bytes 1585160 | tf_op jit(solution)/shard_map/ppermute | solution.py:327
  16.5 23.2 %collective-permute-start.4 = (bf16[1552,128]{1,0:T(8,128)(2,1)S(1)}, bf16[1552,128]{1,0:T(8,128)(2,1)S(1)}, u32[]{:S(2)}, u32[]{:S(2)}) collective-permute-start(bf16[1552,128]{1,0:T(8,128)(2,1)S(1)} %get-tuple-element.23), channel_id=1, source_target_pairs={{0,127},{1,126},{2,1},{3,0},{4,3},{5,2},{6,5},{7,4},{8,7},{9,6},{1... | collective-permute-start | bytes 1191944 | tf_op jit(solution)/shard_map/ppermute | solution.py:327
  25.8 16.0 %collective-permute-start.3 = (bf16[2064,128]{1,0:T(8,128)(2,1)S(1)}, bf16[2064,128]{1,0:T(8,128)(2,1)S(1)}, u32[]{:S(2)}, u32[]{:S(2)}) collective-permute-start(bf16[2064,128]{1,0:T(8,128)(2,1)S(1)} %get-tuple-element.22), channel_id=1, source_target_pairs={{0,126},{1,127},{2,0},{3,1},{4,2},{5,3},{6,4},{7,5},{8,6},{9,7},{1... | collective-permute-start | bytes 1585160 | tf_op jit(solution)/shard_map/ppermute | solution.py:327
  27.6 12.1 %collective-permute-start.7 = (bf16[512,128]{1,0:T(8,128)(2,1)S(1)}, bf16[512,128]{1,0:T(8,128)(2,1)S(1)}, u32[]{:S(2)}, u32[]{:S(2)}) collective-permute-start(bf16[512,128]{1,0:T(8,128)(2,1)S(1)} %collective-permute-done.6), channel_id=1, source_target_pairs={{14,126},{15,127},{46,30},{47,31},{78,62},{79,63},{110,94},{111,95}} | collective-permute-start | bytes 393224 | tf_op jit(solution)/shard_map/ppermute | solution.py:327

commit v2 on v1

--- a/solution.py
+++ b/solution.py
@@ -120,53 +120,67 @@
     half = width // 2
     block = 256
     lanes = 512
-
-    def kernel(rows, far_rows, ids, table, grad, own_table, squares, own_rows, hot, far_hot, sems):
+    token_blocks = tokens // block
+    row_blocks = rows_dev // block
+
+    def kernel(rows, far_rows, ids_in, table, grad, own_table, squares, own_rows, ids, sems):
         vocab, core = own_index()
         own = pl.multiple_of(core * half, half)
         copies = [
             pltpu.make_async_copy(
-                rows.at[:, pl.ds(own + k * lanes, lanes)], own_rows.at[:, pl.ds(k * lanes, lanes)], sems.at[k]
+                rows.at[pl.ds(k * block, block), pl.ds(own, half)], own_rows.at[pl.ds(k * block, block), :], sems.at[k]
             )
-            for k in range(half // lanes)
+            for k in range(token_blocks)
         ]
-        for copy in copies:
-            copy.start()
         table_copies = [
             pltpu.make_async_copy(
-                table.at[:, pl.ds(own + k * LANES, LANES)], own_table.at[k], sems.at[half // lanes]
+                table.at[:, pl.ds(own + k * LANES, LANES)], own_table.at[k], sems.at[token_blocks]
             )
             for k in range(half // LANES)
         ]
-        for copy in table_copies:
+        ids_copy = pltpu.make_async_copy(ids_in, ids, sems.at[token_blocks + 1])
+        for copy in [ids_copy] + copies + table_copies:
             copy.start()
-        start = vocab * rows_dev
+        for k in range(rows_dev // 64):
+            grad[pl.ds(k * 64, 64), :] = jnp.zeros((64, half), jnp.float32)
+
+        def accumulate(local, token_rows, ready):
+            firsts = [local[0, k * block] for k in range(token_blocks)]
+            for k in range(token_blocks):
+                part = local[:, k * block : (k + 1) * block]
+                low = jnp.maximum(lax.shift_right_arithmetic(firsts[k], 8), 0)
+                high = row_blocks - 1
+                if k + 1 < token_blocks:
+                    high = jnp.minimum(lax.shift_right_arithmetic(firsts[k + 1], 8), high)
+                ready(k)
+
+                def step(r, carry):
+                    base = pl.multiple_of(r * block, block)
+                    at = lax.broadcasted_iota(jnp.int32, (block, block), 0) + base
+                    hot = jnp.where(at == part, 1.0, 0.0).astype(jnp.bfloat16)
+                    for c in range(half // lanes):
+                        columns = pl.ds(c * lanes, lanes)
+                        grad[pl.ds(base, block), columns] += jnp.dot(
+                            hot, token_rows[pl.ds(k * block, block), columns], preferred_element_type=jnp.float32
+                        )
+                    return carry
+
+                lax.fori_loop(low, high + 1, step, 0)
+
         sent = far_rows[pl.ds(tokens, TAIL), :].astype(jnp.float32)[:1, :]
-        far_local = joined(sent[:, :tokens], sent[:, tokens:]) - EDGE
-        own_local = jnp.bitwise_and(ids[...] - start, vocab_rows - 1)
-        for one_hot, local in ((hot, own_local), (far_hot, far_local)):
-            for k in range(rows_dev // block):
-                at = lax.broadcasted_iota(jnp.int32, (block, tokens), 0) + k * block
-                one_hot[pl.ds(k * block, block), :] = jnp.where(at == local, 1.0, 0.0).astype(jnp.bfloat16)
-        total = jnp.zeros((1, lanes), jnp.float32)
-        for c in range(half // lanes):
-            copies[c].wait()
-            for r in range(rows_dev // block):
-                part = jnp.dot(
-                    hot[pl.ds(r * block, block), :],
-                    own_rows[:, pl.ds(c * lanes, lanes)],
-                    preferred_element_type=jnp.float32,
-                ) + jnp.dot(
-                    far_hot[pl.ds(r * block, block), :],
-                    far_rows[pl.ds(0, tokens), pl.ds(c * lanes, lanes)],
-                    preferred_element_type=jnp.float32,
-                )
-                grad[pl.ds(r * block, block), pl.ds(c * lanes, lanes)] = part
-                if EDGE <= r * block < rows_dev - EDGE:
-                    total = total + jnp.sum(part * part, axis=0, keepdims=True)
-        fold = total[:, :128]
-        for k in range(1, lanes // 128):
-            fold = fold + total[:, k * 128 : (k + 1) * 128]
+        accumulate(joined(sent[:, :tokens], sent[:, tokens:]) - EDGE, far_rows, lambda k: None)
+        ids_copy.wait()
+        offset = jnp.bitwise_and(ids[...] - vocab * rows_dev + EDGE, vocab_rows - 1)
+        accumulate(offset - EDGE, own_rows, lambda k: copies[k].wait())
+        total = jnp.zeros((8, lanes), jnp.float32)
+        for r in range(EDGE, rows_dev - EDGE, 64):
+            for c in range(half // lanes):
+                value = grad[pl.ds(r, 64), pl.ds(c * lanes, lanes)]
+                total = total + jnp.sum((value * value).reshape(8, 8, lanes), axis=0)
+        total = jnp.sum(total, axis=0, keepdims=True)
+        fold = total[:, :LANES]
+        for k in range(1, lanes // LANES):
+            fold = fold + total[:, k * LANES : (k + 1) * LANES]
         squares[...] = fold
         for copy in table_copies:
             copy.wait()
@@ -176,22 +190,21 @@
         out_shape=[
             pltpu.VMEM((rows_dev, half), jnp.float32),
             pltpu.VMEM((half // LANES, rows_dev, LANES), embed_table.dtype),
-            pltpu.VMEM((1, 128), jnp.float32),
-        ],
-        in_specs=[any_spec(), vmem_spec(), vmem_spec(), any_spec()],
+            pltpu.VMEM((1, LANES), jnp.float32),
+        ],
+        in_specs=[any_spec(), vmem_spec(), any_spec(), any_spec()],
         out_specs=[vmem_spec()] * 3,
         scratch_shapes=[
             pltpu.VMEM((tokens, half), grad_rows.dtype),
-            pltpu.VMEM((rows_dev, tokens), jnp.bfloat16),
-            pltpu.VMEM((rows_dev, tokens), jnp.bfloat16),
-            pltpu.SemaphoreType.DMA((half // lanes + 1,)),
-        ],
-        compiler_params=pltpu.CompilerParams(vmem_limit_bytes=18 * MIB),
+            pltpu.VMEM((1, tokens), jnp.int32),
+            pltpu.SemaphoreType.DMA((token_blocks + 2,)),
+        ],
+        compiler_params=pltpu.CompilerParams(vmem_limit_bytes=12 * MIB),
         cost_estimate=pl.CostEstimate(
             flops=4 * rows_dev * tokens * half, bytes_accessed=8 * MIB, transcendentals=0
         ),
         name="local_gradient",
-    )(in_hbm(grad_rows), in_vmem(swapped), own_ids, in_hbm(embed_table))
+    )(in_hbm(grad_rows), in_vmem(swapped), in_hbm(own_ids), in_hbm(embed_table))
 
 
 def edge_gradient(grad, squares, same, cross, rest, side, spread_rows):
@@ -331,7 +344,7 @@
 
     last = token_ids.shape[1] - TOK_EDGE
     tiles = width // replicas // LANES
-    kept = tiles - tiles // 4
+    kept = tiles - 3
     shape = (rows_dev, vocab_rows)
     plus_same, minus_same, minus_rest = pack(
         rows,

time: 63.7 us -> 64.4 us (1.011)
  waiting for transfers between devices: 6.22 us -> 10.5 us
  Pallas kernels: 18.4 us -> 14.9 us
    ppermute x8, waiting for transfers between devices: 6.22 us -> 10.5 us  [moved(): return lax.ppermute(piece, VOCAB_DP, pairs)]
    pallas_call x1, Pallas kernels: 10.7 us -> 7.18 us  [local_gradient(): pl.pallas_call(kernel, out_shape=[pltpu.VMEM((rows_dev, half), jnp.float3...]
  transfers between devices with their start and end apart: 8 -> 8, of which waited for: 2 -> 3; matrix products, arithmetic and copies ran while one was open for 0% -> 0% of each run, Pallas kernels for 20% -> 14%
where the time goes in v2:
time: 64.4 us; the launch traced here: 64.2 us
  starting transfers between devices  19.5 us (30%)
  blocking collectives  18.6 us (29%)
  Pallas kernels  14.9 us (23%)
  waiting for transfers between devices  10.5 us (16%)
  between operations  0.72 us (1%)
    ppermute x8, starting transfers between devices, moved(): return lax.ppermute(piece, VOCAB_DP, pairs)  19.5 us
    all_to_all x1, blocking collectives, body(): partials = lax.all_to_all(spread, VOCAB_DP, 0, 0, tiled=True)  18.6 us
    ppermute x8, waiting for transfers between devices, moved(): return lax.ppermute(piece, VOCAB_DP, pairs)  10.5 us
    pallas_call x1, Pallas kernels, local_gradient(): pl.pallas_call(kernel, out_shape=[pltpu.VMEM((rows_dev, half), jnp.float3...  7.18 us
    pallas_call x2, Pallas kernels, pack(): pl.pallas_call(kernel, out_shape=shapes, in_specs=[any_spec(), any_spec()...  3.87 us
    pallas_call x1, Pallas kernels, clipped_update(): pl.pallas_call(kernel, out_shape=[jax.ShapeDtypeStruct((rows_dev, half),...  2.34 us
    pallas_call x2, Pallas kernels, edge_gradient(): pl.pallas_call(kernel, out_shape=[pltpu.VMEM((rows_dev, half), jnp.float3...  1.48 us
  transfers between devices with their start and end apart: 8, of which 3 were waited for; matrix products, arithmetic and copies ran while one was open for 0% of the time, Pallas kernels for 14%

profile of v2, /device:TPU:1, one launch (start us, length us, event | category | flops | bytes accessed | tf_op | source)
XLA Modules:
  0.0 64.2 jit_solution(15898791194227954007)
XLA Ops:
  0.6 2.6 %shard_map.50 = (bf16[2064,128]{1,0:T(8,128)(2,1)S(1)}, bf16[1680,128]{1,0:T(8,128)(2,1)S(1)}, bf16[1040,2048]{1,0:T(8,128)(2,1)S(1)}) custom-call(bf16[1024,4096]{1,0:T(8,128)(2,1)} %bitcast.7, s32[1,1024]{1,0:T(1,128)} %ids_in.5), custom_call_target="tpu_custom_call" | custom-call | tf_op jit(solution)/shard_map/pallas_call | solution.py:107
  3.3 1.5 %collective-permute-start = (bf16[1040,2048]{1,0:T(8,128)(2,1)S(1)}, bf16[1040,2048]{1,0:T(8,128)(2,1)S(1)}, u32[]{:S(2)}, u32[]{:S(2)}) collective-permute-start(bf16[1040,2048]{1,0:T(8,128)(2,1)S(1)} %get-tuple-element.15), channel_id=1, source_target_pairs={{0,1},{1,0},{2,3},{3,2},{4,5},{5,4},{6,7},{7,6},{8,9},{9,8},{10,11... | collective-permute-start | bytes 12779528 | tf_op jit(solution)/shard_map/ppermute | solution.py:340
  4.7 1.7 %collective-permute-start.2 = (bf16[2064,128]{1,0:T(8,128)(2,1)S(1)}, bf16[2064,128]{1,0:T(8,128)(2,1)S(1)}, u32[]{:S(2)}, u32[]{:S(2)}) collective-permute-start(bf16[2064,128]{1,0:T(8,128)(2,1)S(1)} %get-tuple-element.19), channel_id=1, source_target_pairs={{0,3},{1,2},{2,5},{3,4},{4,7},{5,6},{6,9},{7,8},{8,11},{9,10},{10,... | collective-permute-start | bytes 1585160 | tf_op jit(solution)/shard_map/ppermute | solution.py:340
  6.4 1.2 %shard_map.51 = (bf16[2064,128]{1,0:T(8,128)(2,1)S(1)}, bf16[2064,128]{1,0:T(8,128)(2,1)S(1)}, bf16[384,128]{1,0:T(8,128)(2,1)S(1)}) custom-call(bf16[1024,4096]{1,0:T(8,128)(2,1)} %bitcast.8, s32[1,1024]{1,0:T(1,128)} %ids_in.5), custom_call_target="tpu_custom_call" | custom-call | tf_op jit(solution)/shard_map/pallas_call | solution.py:107
  7.7 5.3 %collective-permute-start.6 = (bf16[384,128]{1,0:T(8,128)(2,1)S(1)}, bf16[384,128]{1,0:T(8,128)(2,1)S(1)}, u32[]{:S(2)}, u32[]{:S(2)}) collective-permute-start(bf16[384,128]{1,0:T(8,128)(2,1)S(1)} %get-tuple-element.24), channel_id=1, source_target_pairs={{0,15},{1,14},{32,47},{33,46},{64,79},{65,78},{96,111},{97,110}} | collective-permute-start | bytes 294920 | tf_op jit(solution)/shard_map/ppermute | solution.py:340
  13.0 1.3 %collective-permute-start.5 = (bf16[384,128]{1,0:T(8,128)(2,1)S(1)}, bf16[384,128]{1,0:T(8,128)(2,1)S(1)}, u32[]{:S(2)}, u32[]{:S(2)}) collective-permute-start(bf16[384,128]{1,0:T(8,128)(2,1)S(1)} %get-tuple-element.24), channel_id=1, source_target_pairs={{2,1},{3,0},{4,3},{5,2},{6,5},{7,4},{8,7},{9,6},{10,9},{11,8},{12,... | collective-permute-start | bytes 294920 | tf_op jit(solution)/shard_map/ppermute | solution.py:340
  14.3 2.2 %collective-permute-start.1 = (bf16[2064,128]{1,0:T(8,128)(2,1)S(1)}, bf16[2064,128]{1,0:T(8,128)(2,1)S(1)}, u32[]{:S(2)}, u32[]{:S(2)}) collective-permute-start(bf16[2064,128]{1,0:T(8,128)(2,1)S(1)} %get-tuple-element.18), channel_id=1, source_target_pairs={{0,2},{1,3},{2,4},{3,5},{4,6},{5,7},{6,8},{7,9},{8,10},{9,11},{10,... | collective-permute-start | bytes 1585160 | tf_op jit(solution)/shard_map/ppermute | solution.py:340
  16.5 0.0 collective-permute-done.6
  16.5 5.1 %collective-permute-start.4 = (bf16[1680,128]{1,0:T(8,128)(2,1)S(1)}, bf16[1680,128]{1,0:T(8,128)(2,1)S(1)}, u32[]{:S(2)}, u32[]{:S(2)}) collective-permute-start(bf16[1680,128]{1,0:T(8,128)(2,1)S(1)} %get-tuple-element.23), channel_id=1, source_target_pairs={{0,127},{1,126},{2,1},{3,0},{4,3},{5,2},{6,5},{7,4},{8,7},{9,6},{1... | collective-permute-start | bytes 1290248 | tf_op jit(solution)/shard_map/ppermute | solution.py:340
  21.6 4.2 %collective-permute-done.2.cross = bf16[2064,128]{1,0:T(8,128)(2,1)S(1)} collective-permute-done((bf16[2064,128]{1,0:T(8,128)(2,1)S(1)}, bf16[2064,128]{1,0:T(8,128)(2,1)S(1)}, u32[]{:S(2)}, u32[]{:S(2)}) %collective-permute-start.2) | collective-permute-done | bytes 528416 | tf_op jit(solution)/shard_map/ppermute | solution.py:340
  25.8 1.8 %collective-permute-start.3 = (bf16[2064,128]{1,0:T(8,128)(2,1)S(1)}, bf16[2064,128]{1,0:T(8,128)(2,1)S(1)}, u32[]{:S(2)}, u32[]{:S(2)}) collective-permute-start(bf16[2064,128]{1,0:T(8,128)(2,1)S(1)} %get-tuple-element.22), channel_id=1, source_target_pairs={{0,126},{1,127},{2,0},{3,1},{4,2},{5,3},{6,4},{7,5},{8,6},{9,7},{1... | collective-permute-start | bytes 1585160 | tf_op jit(solution)/shard_map/ppermute | solution.py:340
  27.5 0.0 collective-permute-done.far_rows
  27.5 0.7 %collective-permute-start.7 = (bf16[384,128]{1,0:T(8,128)(2,1)S(1)}, bf16[384,128]{1,0:T(8,128)(2,1)S(1)}, u32[]{:S(2)}, u32[]{:S(2)}) collective-permute-start(bf16[384,128]{1,0:T(8,128)(2,1)S(1)} %collective-permute-done.6), channel_id=1, source_target_pairs={{14,126},{15,127},{46,30},{47,31},{78,62},{79,63},{110,94},{111,95}} | collective-permute-start | bytes 294920 | tf_op jit(solution)/shard_map/ppermute | solution.py:340
  28.2 7.2 %local_gradient.1 = (f32[1024,2048]{1,0:T(8,128)S(1)}, bf16[16,1024,128]{2,1,0:T(8,128)(2,1)S(1)}, f32[1,128]{1,0:T(1,128)S(1)}) custom-call(bf16[1024,4096]{1,0:T(8,128)(2,1)} %bitcast.9, bf16[1040,2048]{1,0:T(8,128)(2,1)S(1)} %collective-permute-done.far_rows, s32[1,1024]{1,0:T(1,128)} %ids_in.5, bf16[1024,4096]{1,0:T(8,128)(2,1)} %table.1), custom_call_target="tpu_custom_call" | custom-call | flops 8589934592 | bytes 8388608 | tf_op jit(solution)/shard_map/local_gradient/pallas_call | solution.py:188
  35.4 1.5 %collective-permute-done.1.same = bf16[2064,128]{1,0:T(8,128)(2,1)S(1)} collective-permute-done((bf16[2064,128]{1,0:T(8,128)(2,1)S(1)}, bf16[2064,128]{1,0:T(8,128)(2,1)S(1)}, u32[]{:S(2)}, u32[]{:S(2)}) %collective-permute-start.1) | collective-permute-done | bytes 528416 | tf_op jit(solution)/shard_map/ppermute | solution.py:340
  36.9 0.7 %shard_map.52 = (f32[1024,2048]{1,0:T(8,128)S(1)}, f32[1,128]{1,0:T(1,128)S(1)}) custom-call(f32[1024,2048]{1,0:T(8,128)S(1)} %get-tuple-element.16.grad_in, f32[1,128]{1,0:T(1,128)S(1)} %get-tuple-element.17.squares_in, bf16[2064,128]{1,0:T(8,128)(2,1)S(1)} %collective-permute-done.1.same, ...), custom_call_target="tpu_custom_call", output_to_operand_aliasing={{0}: (0, {})} | custom-call | flops 268435456 | bytes 2097152 | tf_op jit(solution)/shard_map/pallas_call | solution.py:257
  37.6 0.0 collective-permute-done.5.refs_0_
  37.6 0.0 collective-permute-done.7.refs_1_
  37.6 0.0 collective-permute-done.4.cross
  37.6 4.8 %collective-permute-done.3.same = bf16[2064,128]{1,0:T(8,128)(2,1)S(1)} collective-permute-done((bf16[2064,128]{1,0:T(8,128)(2,1)S(1)}, bf16[2064,128]{1,0:T(8,128)(2,1)S(1)}, u32[]{:S(2)}, u32[]{:S(2)}) %collective-permute-start.3) | collective-permute-done | bytes 528416 | tf_op jit(solution)/shard_map/ppermute | solution.py:340
  42.4 0.8 %shard_map.53 = (f32[1024,2048]{1,0:T(8,128)S(1)}, f32[128,128]{1,0:T(8,128)S(1)}) custom-call(f32[1024,2048]{1,0:T(8,128)S(1)} %get-tuple-element.20.grad_in, f32[1,128]{1,0:T(1,128)S(1)} %get-tuple-element.21.squares_in, bf16[2064,128]{1,0:T(8,128)(2,1)S(1)} %collective-permute-done.3.same, ...), custom_call_target="tpu_custom_call", output_to_operand_aliasing={{0}: (0, {})} | custom-call | flops 268435456 | bytes 2097152 | tf_op jit(solution)/shard_map/pallas_call | solution.py:257
  43.2 18.6 %all_to_all.11 = f32[128,1,128]{2,1,0:T(1,128)S(1)} all-to-all(f32[128,1,128]{2,1,0:T(1,128)S(1)} %bitcast.6), channel_id=1, replica_groups=mesh['vocab_0'=4,'vocab_1'=4,'vocab_2'=4,'dp'=2] {'vocab_0','vocab_1','v..., dimensions={0} | all-to-all | bytes 131072 | tf_op jit(solution)/shard_map/all_to_all | solution.py:374
  61.8 2.3 %clipped_update.1 = (bf16[1024,2048]{1,0:T(8,128)(2,1)}, f32[1]{0:T(128)}) custom-call(f32[1024,2048]{1,0:T(8,128)S(1)} %get-tuple-element.25.grad_in, bf16[16,1024,128]{2,1,0:T(8,128)(2,1)S(1)} %get-tuple-element.26.table_in, f32[128,128]{1,0:T(8,128)S(1)} %bitcast.5), custom_call_target="tpu_custom_call" | custom-call | tf_op jit(solution)/shard_map/clipped_update/pallas_call | solution.py:296
Async XLA Ops:
  3.3 24.3 %collective-permute-start = (bf16[1040,2048]{1,0:T(8,128)(2,1)S(1)}, bf16[1040,2048]{1,0:T(8,128)(2,1)S(1)}, u32[]{:S(2)}, u32[]{:S(2)}) collective-permute-start(bf16[1040,2048]{1,0:T(8,128)(2,1)S(1)} %get-tuple-element.15), channel_id=1, source_target_pairs={{0,1},{1,0},{2,3},{3,2},{4,5},{5,4},{6,7},{7,6},{8,9},{9,8},{10,11... | collective-permute-start | bytes 12779528 | tf_op jit(solution)/shard_map/ppermute | solution.py:340
  4.7 21.1 %collective-permute-start.2 = (bf16[2064,128]{1,0:T(8,128)(2,1)S(1)}, bf16[2064,128]{1,0:T(8,128)(2,1)S(1)}, u32[]{:S(2)}, u32[]{:S(2)}) collective-permute-start(bf16[2064,128]{1,0:T(8,128)(2,1)S(1)} %get-tuple-element.19), channel_id=1, source_target_pairs={{0,3},{1,2},{2,5},{3,4},{4,7},{5,6},{6,9},{7,8},{8,11},{9,10},{10,... | collective-permute-start | bytes 1585160 | tf_op jit(solution)/shard_map/ppermute | solution.py:340
  7.7 8.8 %collective-permute-start.6 = (bf16[384,128]{1,0:T(8,128)(2,1)S(1)}, bf16[384,128]{1,0:T(8,128)(2,1)S(1)}, u32[]{:S(2)}, u32[]{:S(2)}) collective-permute-start(bf16[384,128]{1,0:T(8,128)(2,1)S(1)} %get-tuple-element.24), channel_id=1, source_target_pairs={{0,15},{1,14},{32,47},{33,46},{64,79},{65,78},{96,111},{97,110}} | collective-permute-start | bytes 294920 | tf_op jit(solution)/shard_map/ppermute | solution.py:340
  13.0 24.6 %collective-permute-start.5 = (bf16[384,128]{1,0:T(8,128)(2,1)S(1)}, bf16[384,128]{1,0:T(8,128)(2,1)S(1)}, u32[]{:S(2)}, u32[]{:S(2)}) collective-permute-start(bf16[384,128]{1,0:T(8,128)(2,1)S(1)} %get-tuple-element.24), channel_id=1, source_target_pairs={{2,1},{3,0},{4,3},{5,2},{6,5},{7,4},{8,7},{9,6},{10,9},{11,8},{12,... | collective-permute-start | bytes 294920 | tf_op jit(solution)/shard_map/ppermute | solution.py:340
  14.3 22.6 %collective-permute-start.1 = (bf16[2064,128]{1,0:T(8,128)(2,1)S(1)}, bf16[2064,128]{1,0:T(8,128)(2,1)S(1)}, u32[]{:S(2)}, u32[]{:S(2)}) collective-permute-start(bf16[2064,128]{1,0:T(8,128)(2,1)S(1)} %get-tuple-element.18), channel_id=1, source_target_pairs={{0,2},{1,3},{2,4},{3,5},{4,6},{5,7},{6,8},{7,9},{8,10},{9,11},{10,... | collective-permute-start | bytes 1585160 | tf_op jit(solution)/shard_map/ppermute | solution.py:340
  16.5 21.1 %collective-permute-start.4 = (bf16[1680,128]{1,0:T(8,128)(2,1)S(1)}, bf16[1680,128]{1,0:T(8,128)(2,1)S(1)}, u32[]{:S(2)}, u32[]{:S(2)}) collective-permute-start(bf16[1680,128]{1,0:T(8,128)(2,1)S(1)} %get-tuple-element.23), channel_id=1, source_target_pairs={{0,127},{1,126},{2,1},{3,0},{4,3},{5,2},{6,5},{7,4},{8,7},{9,6},{1... | collective-permute-start | bytes 1290248 | tf_op jit(solution)/shard_map/ppermute | solution.py:340
  25.8 16.7 %collective-permute-start.3 = (bf16[2064,128]{1,0:T(8,128)(2,1)S(1)}, bf16[2064,128]{1,0:T(8,128)(2,1)S(1)}, u32[]{:S(2)}, u32[]{:S(2)}) collective-permute-start(bf16[2064,128]{1,0:T(8,128)(2,1)S(1)} %get-tuple-element.22), channel_id=1, source_target_pairs={{0,126},{1,127},{2,0},{3,1},{4,2},{5,3},{6,4},{7,5},{8,6},{9,7},{1... | collective-permute-start | bytes 1585160 | tf_op jit(solution)/shard_map/ppermute | solution.py:340
  27.5 10.0 %collective-permute-start.7 = (bf16[384,128]{1,0:T(8,128)(2,1)S(1)}, bf16[384,128]{1,0:T(8,128)(2,1)S(1)}, u32[]{:S(2)}, u32[]{:S(2)}) collective-permute-start(bf16[384,128]{1,0:T(8,128)(2,1)S(1)} %collective-permute-done.6), channel_id=1, source_target_pairs={{14,126},{15,127},{46,30},{47,31},{78,62},{79,63},{110,94},{111,95}} | collective-permute-start | bytes 294920 | tf_op jit(solution)/shard_map/ppermute | solution.py:340

commit v3 on v2

--- a/solution.py
+++ b/solution.py
@@ -207,24 +207,14 @@
     )(in_hbm(grad_rows), in_vmem(swapped), in_hbm(own_ids), in_hbm(embed_table))
 
 
-def edge_gradient(grad, squares, same, cross, rest, side, spread_rows):
-    rows_dev, half = grad.shape
+def edge_gradient(grad, squares, same, cross, rest, side, tiles, spread_rows):
+    rows_dev = grad.shape[0]
     group = 4
-    lanes = group * LANES
     base = rows_dev - EDGE if side < 0 else 0
     first = 0 if side < 0 else rows_dev + EDGE
 
     def kernel(grad_in, squares_in, same, cross, *refs):
         others, (grad_out, spread) = refs[:-2], refs[-2:]
-
-        def tile(part, k):
-            whole = part.shape[0] // TOK_EDGE
-            if k < whole:
-                return part[pl.ds(k * TOK_EDGE, TOK_EDGE), :]
-            rows = pl.ds((k - whole) * TOK_EDGE, TOK_EDGE)
-            return others[0][rows, :] + others[1][rows, :]
-
-        total = jnp.zeros((8, lanes), jnp.float32)
         at = lax.broadcasted_iota(jnp.int32, (EDGE, TOK_EDGE), 0) + first
         hot = []
         for part in (same, cross):
@@ -232,14 +222,24 @@
             offset = joined(sent[:1, :], sent[TAIL // 2 : TAIL // 2 + 1, :])
             hot.append(jnp.where(at == offset, 1.0, 0.0).astype(jnp.bfloat16))
         hot = jnp.concatenate(hot, axis=1)
-        for c in range(half // lanes):
-            columns = pl.ds(c * lanes, lanes)
+
+        def same_tile(k):
+            return same[pl.ds(k * TOK_EDGE, TOK_EDGE), :]
+
+        def cross_tile(k):
+            if not others:
+                return cross[pl.ds(k * TOK_EDGE, TOK_EDGE), :]
+            rows = pl.ds((k - tiles[0]) * TOK_EDGE, TOK_EDGE)
+            return others[0][rows, :] + others[1][rows, :]
+
+        total = jnp.zeros((8, LANES), jnp.float32)
+        for low in range(tiles[0], tiles[1], group):
+            span = range(low, min(low + group, tiles[1]))
+            columns = pl.ds(low * LANES, len(span) * LANES)
             rows = jnp.concatenate(
                 [
-                    jnp.concatenate(
-                        [tile(part, c * group + g) for g in range(group)], axis=1
-                    )
-                    for part in (same, cross)
+                    jnp.concatenate([tile(k) for k in span], axis=1)
+                    for tile in (same_tile, cross_tile)
                 ],
                 axis=0,
             )
@@ -247,24 +247,25 @@
                 hot, rows, preferred_element_type=jnp.float32
             )
             grad_out[pl.ds(base, EDGE), columns] = value
-            total = total + jnp.sum((value * value).reshape(EDGE // 8, 8, lanes), axis=0)
-        total = jnp.sum(total, axis=0, keepdims=True)
-        fold = squares_in[...]
-        for k in range(group):
-            fold = fold + total[:, k * LANES : (k + 1) * LANES]
+            square = jnp.sum((value * value).reshape(EDGE // 8, 8, len(span) * LANES), axis=0)
+            for k in range(len(span)):
+                total = total + square[:, k * LANES : (k + 1) * LANES]
+        fold = squares_in[...] + jnp.sum(total, axis=0, keepdims=True)
         spread[...] = jnp.broadcast_to(fold, (spread_rows, LANES))
 
     return pl.pallas_call(
         kernel,
         out_shape=[
-            pltpu.VMEM((rows_dev, half), jnp.float32),
+            pltpu.VMEM(grad.shape, jnp.float32),
             pltpu.VMEM((spread_rows, LANES), jnp.float32),
         ],
         in_specs=[vmem_spec()] * (4 + len(rest)),
         out_specs=[vmem_spec()] * 2,
         input_output_aliases={0: 0},
         compiler_params=pltpu.CompilerParams(vmem_limit_bytes=4 * MIB),
-        cost_estimate=pl.CostEstimate(flops=4 * EDGE * TOK_EDGE * half, bytes_accessed=2 * MIB, transcendentals=0),
+        cost_estimate=pl.CostEstimate(
+            flops=4 * EDGE * TOK_EDGE * (tiles[1] - tiles[0]) * LANES, bytes_accessed=2 * MIB, transcendentals=0
+        ),
     )(in_vmem(grad), in_vmem(squares), in_vmem(same), in_vmem(cross), *[in_vmem(part) for part in rest])
 
 
@@ -330,10 +331,13 @@
     plane = vocab_count // lax.axis_size(VOCAB[0])
     line = lax.axis_size(VOCAB[2])
     corners = range(0, vocab_count, plane)
-    relays = {v: v + 2 * line - 1 for v in corners}
-    to_relay = [(v * replicas + p, relays[v] * replicas + 1 - p) for v in corners for p in range(replicas)]
+    relays = {}
+    for v in corners:
+        relays[v, 0] = (v + 2 * line - 1, 1)
+        relays[v, 1] = ((v + plane + line - 1) % vocab_count, 0)
+    to_relay = [(v * replicas + p, w * replicas + q) for (v, p), (w, q) in relays.items()]
     from_relay = [
-        (relays[v] * replicas + p, (v - 1) % vocab_count * replicas + p) for v in corners for p in range(replicas)
+        (w * replicas + q, (v - 1) % vocab_count * replicas + q) for (v, _), (w, q) in relays.items()
     ]
 
     def moved(piece, pairs):
@@ -344,7 +348,7 @@
 
     last = token_ids.shape[1] - TOK_EDGE
     tiles = width // replicas // LANES
-    kept = tiles - 3
+    kept = tiles - 5
     shape = (rows_dev, vocab_rows)
     plus_same, minus_same, minus_rest = pack(
         rows,
@@ -359,18 +363,21 @@
     )
     plus_same = sent(plus_same, 1, False)
     minus_same = sent(minus_same, -1, False)
-    relayed = moved(minus_rest, to_relay)
     plus_cross, minus_cross, far = pack(
         rows, token_ids, *shape, ((last, True, 0, tiles, True), (0, True, 0, kept, True)), True
     )
     far = sent(far, 0, True)
     minus_cross = sent(minus_cross, -1, True)
     plus_cross = sent(plus_cross, 1, True)
+    relayed = moved(minus_rest, to_relay)
     minus_rest = sent(minus_rest, -1, True, corners)
     relayed = moved(relayed, from_relay)
     grad, own_table, squares = local_gradient(rows, far, token_ids, embed_table, vocab_rows)
-    grad, squares = edge_gradient(grad, squares, plus_same, plus_cross, (), 1, 1)
-    grad, spread = edge_gradient(grad, squares, minus_same, minus_cross, (minus_rest, relayed), -1, devices)
+    grad, squares = edge_gradient(grad, squares, plus_same, plus_cross, (), 1, (0, tiles), 1)
+    grad, squares = edge_gradient(grad, squares, minus_same, minus_cross, (), -1, (0, kept), 1)
+    grad, spread = edge_gradient(
+        grad, squares, minus_same, minus_cross, (minus_rest, relayed), -1, (kept, tiles), devices
+    )
     partials = lax.all_to_all(spread, VOCAB_DP, 0, 0, tiled=True)
     return tuple(clipped_update(grad, own_table, partials, vocab_rows * width))
 

time: 64.4 us -> 63.3 us (0.983)
  waiting for transfers between devices: 10.5 us -> 9.16 us
    ppermute x8, waiting for transfers between devices: 10.5 us -> 9.16 us  [moved(): return lax.ppermute(piece, VOCAB_DP, pairs)]
    pallas_call x2 -> x3, Pallas kernels: 1.48 us -> 1.69 us  [edge_gradient(): pl.pallas_call(kernel, out_shape=[pltpu.VMEM(grad.shape, jnp.float32), pl...]
  transfers between devices with their start and end apart: 8 -> 8, of which waited for: 3 -> 3; matrix products, arithmetic and copies ran while one was open for 0% -> 0% of each run, Pallas kernels for 14% -> 15%
where the time goes in v3:
time: 63.3 us; the launch traced here: 63 us
  starting transfers between devices  19.5 us (31%)
  blocking collectives  18.5 us (29%)
  Pallas kernels  15.1 us (24%)
  waiting for transfers between devices  9.16 us (14%)
  between operations  0.71 us (1%)
    ppermute x8, starting transfers between devices, moved(): return lax.ppermute(piece, VOCAB_DP, pairs)  19.5 us
    all_to_all x1, blocking collectives, body(): partials = lax.all_to_all(spread, VOCAB_DP, 0, 0, tiled=True)  18.5 us
    ppermute x8, waiting for transfers between devices, moved(): return lax.ppermute(piece, VOCAB_DP, pairs)  9.16 us
    pallas_call x1, Pallas kernels, local_gradient(): pl.pallas_call(kernel, out_shape=[pltpu.VMEM((rows_dev, half), jnp.float3...  7.18 us
    pallas_call x2, Pallas kernels, pack(): pl.pallas_call(kernel, out_shape=shapes, in_specs=[any_spec(), any_spec()...  3.87 us
    pallas_call x1, Pallas kernels, clipped_update(): pl.pallas_call(kernel, out_shape=[jax.ShapeDtypeStruct((rows_dev, half),...  2.34 us
    pallas_call x3, Pallas kernels, edge_gradient(): pl.pallas_call(kernel, out_shape=[pltpu.VMEM(grad.shape, jnp.float32), pl...  1.69 us
  transfers between devices with their start and end apart: 8, of which 3 were waited for; matrix products, arithmetic and copies ran while one was open for 0% of the time, Pallas kernels for 15%

profile of v3, /device:TPU:1, one launch (start us, length us, event | category | flops | bytes accessed | tf_op | source)
XLA Modules:
  0.0 63.0 jit_solution(4624858344780581978)
XLA Ops:
  0.6 2.6 %shard_map.50 = (bf16[2064,128]{1,0:T(8,128)(2,1)S(1)}, bf16[1424,128]{1,0:T(8,128)(2,1)S(1)}, bf16[1040,2048]{1,0:T(8,128)(2,1)S(1)}) custom-call(bf16[1024,4096]{1,0:T(8,128)(2,1)} %bitcast.7, s32[1,1024]{1,0:T(1,128)} %ids_in.5), custom_call_target="tpu_custom_call" | custom-call | tf_op jit(solution)/shard_map/pallas_call | solution.py:107
  3.2 1.5 %collective-permute-start = (bf16[1040,2048]{1,0:T(8,128)(2,1)S(1)}, bf16[1040,2048]{1,0:T(8,128)(2,1)S(1)}, u32[]{:S(2)}, u32[]{:S(2)}) collective-permute-start(bf16[1040,2048]{1,0:T(8,128)(2,1)S(1)} %get-tuple-element.17), channel_id=1, source_target_pairs={{0,1},{1,0},{2,3},{3,2},{4,5},{5,4},{6,7},{7,6},{8,9},{9,8},{10,11... | collective-permute-start | bytes 12779528 | tf_op jit(solution)/shard_map/ppermute | solution.py:344
  4.7 1.7 %collective-permute-start.2 = (bf16[2064,128]{1,0:T(8,128)(2,1)S(1)}, bf16[2064,128]{1,0:T(8,128)(2,1)S(1)}, u32[]{:S(2)}, u32[]{:S(2)}) collective-permute-start(bf16[2064,128]{1,0:T(8,128)(2,1)S(1)} %get-tuple-element.21), channel_id=1, source_target_pairs={{0,3},{1,2},{2,5},{3,4},{4,7},{5,6},{6,9},{7,8},{8,11},{9,10},{10,... | collective-permute-start | bytes 1585160 | tf_op jit(solution)/shard_map/ppermute | solution.py:344
  6.4 1.3 %shard_map.51 = (bf16[2064,128]{1,0:T(8,128)(2,1)S(1)}, bf16[2064,128]{1,0:T(8,128)(2,1)S(1)}, bf16[640,128]{1,0:T(8,128)(2,1)S(1)}) custom-call(bf16[1024,4096]{1,0:T(8,128)(2,1)} %bitcast.8, s32[1,1024]{1,0:T(1,128)} %ids_in.5), custom_call_target="tpu_custom_call" | custom-call | tf_op jit(solution)/shard_map/pallas_call | solution.py:107
  7.7 5.2 %collective-permute-start.6 = (bf16[640,128]{1,0:T(8,128)(2,1)S(1)}, bf16[640,128]{1,0:T(8,128)(2,1)S(1)}, u32[]{:S(2)}, u32[]{:S(2)}) collective-permute-start(bf16[640,128]{1,0:T(8,128)(2,1)S(1)} %get-tuple-element.28), channel_id=1, source_target_pairs={{0,15},{1,38},{32,47},{33,70},{64,79},{65,102},{96,111},{97,6}} | collective-permute-start | bytes 491528 | tf_op jit(solution)/shard_map/ppermute | solution.py:344
  12.9 1.3 %collective-permute-start.5 = (bf16[640,128]{1,0:T(8,128)(2,1)S(1)}, bf16[640,128]{1,0:T(8,128)(2,1)S(1)}, u32[]{:S(2)}, u32[]{:S(2)}) collective-permute-start(bf16[640,128]{1,0:T(8,128)(2,1)S(1)} %get-tuple-element.28), channel_id=1, source_target_pairs={{2,1},{3,0},{4,3},{5,2},{6,5},{7,4},{8,7},{9,6},{10,9},{11,8},{12,... | collective-permute-start | bytes 491528 | tf_op jit(solution)/shard_map/ppermute | solution.py:344
  14.2 2.3 %collective-permute-start.1 = (bf16[2064,128]{1,0:T(8,128)(2,1)S(1)}, bf16[2064,128]{1,0:T(8,128)(2,1)S(1)}, u32[]{:S(2)}, u32[]{:S(2)}) collective-permute-start(bf16[2064,128]{1,0:T(8,128)(2,1)S(1)} %get-tuple-element.20), channel_id=1, source_target_pairs={{0,2},{1,3},{2,4},{3,5},{4,6},{5,7},{6,8},{7,9},{8,10},{9,11},{10,... | collective-permute-start | bytes 1585160 | tf_op jit(solution)/shard_map/ppermute | solution.py:344
  16.5 0.0 collective-permute-done.6
  16.5 5.1 %collective-permute-start.4 = (bf16[1424,128]{1,0:T(8,128)(2,1)S(1)}, bf16[1424,128]{1,0:T(8,128)(2,1)S(1)}, u32[]{:S(2)}, u32[]{:S(2)}) collective-permute-start(bf16[1424,128]{1,0:T(8,128)(2,1)S(1)} %get-tuple-element.25), channel_id=1, source_target_pairs={{0,127},{1,126},{2,1},{3,0},{4,3},{5,2},{6,5},{7,4},{8,7},{9,6},{1... | collective-permute-start | bytes 1093640 | tf_op jit(solution)/shard_map/ppermute | solution.py:344
  21.6 4.1 %collective-permute-done.2.cross = bf16[2064,128]{1,0:T(8,128)(2,1)S(1)} collective-permute-done((bf16[2064,128]{1,0:T(8,128)(2,1)S(1)}, bf16[2064,128]{1,0:T(8,128)(2,1)S(1)}, u32[]{:S(2)}, u32[]{:S(2)}) %collective-permute-start.2) | collective-permute-done | bytes 528416 | tf_op jit(solution)/shard_map/ppermute | solution.py:344
  25.8 1.8 %collective-permute-start.3 = (bf16[2064,128]{1,0:T(8,128)(2,1)S(1)}, bf16[2064,128]{1,0:T(8,128)(2,1)S(1)}, u32[]{:S(2)}, u32[]{:S(2)}) collective-permute-start(bf16[2064,128]{1,0:T(8,128)(2,1)S(1)} %get-tuple-element.24), channel_id=1, source_target_pairs={{0,126},{1,127},{2,0},{3,1},{4,2},{5,3},{6,4},{7,5},{8,6},{9,7},{1... | collective-permute-start | bytes 1585160 | tf_op jit(solution)/shard_map/ppermute | solution.py:344
  27.5 0.0 collective-permute-done.far_rows
  27.5 0.7 %collective-permute-start.7 = (bf16[640,128]{1,0:T(8,128)(2,1)S(1)}, bf16[640,128]{1,0:T(8,128)(2,1)S(1)}, u32[]{:S(2)}, u32[]{:S(2)}) collective-permute-start(bf16[640,128]{1,0:T(8,128)(2,1)S(1)} %collective-permute-done.6), channel_id=1, source_target_pairs={{15,127},{38,126},{47,31},{70,30},{79,63},{102,62},{111,95},{6,94}} | collective-permute-start | bytes 491528 | tf_op jit(solution)/shard_map/ppermute | solution.py:344
  28.2 7.2 %local_gradient.1 = (f32[1024,2048]{1,0:T(8,128)S(1)}, bf16[16,1024,128]{2,1,0:T(8,128)(2,1)S(1)}, f32[1,128]{1,0:T(1,128)S(1)}) custom-call(bf16[1024,4096]{1,0:T(8,128)(2,1)} %bitcast.9, bf16[1040,2048]{1,0:T(8,128)(2,1)S(1)} %collective-permute-done.far_rows, s32[1,1024]{1,0:T(1,128)} %ids_in.5, bf16[1024,4096]{1,0:T(8,128)(2,1)} %table.1), custom_call_target="tpu_custom_call" | custom-call | flops 8589934592 | bytes 8388608 | tf_op jit(solution)/shard_map/local_gradient/pallas_call | solution.py:188
  35.4 1.5 %collective-permute-done.1.same = bf16[2064,128]{1,0:T(8,128)(2,1)S(1)} collective-permute-done((bf16[2064,128]{1,0:T(8,128)(2,1)S(1)}, bf16[2064,128]{1,0:T(8,128)(2,1)S(1)}, u32[]{:S(2)}, u32[]{:S(2)}) %collective-permute-start.1) | collective-permute-done | bytes 528416 | tf_op jit(solution)/shard_map/ppermute | solution.py:344
  36.8 0.7 %shard_map.52 = (f32[1024,2048]{1,0:T(8,128)S(1)}, f32[1,128]{1,0:T(1,128)S(1)}) custom-call(f32[1024,2048]{1,0:T(8,128)S(1)} %get-tuple-element.18.grad_in, f32[1,128]{1,0:T(1,128)S(1)} %get-tuple-element.19.squares_in, bf16[2064,128]{1,0:T(8,128)(2,1)S(1)} %collective-permute-done.1.same, ...), custom_call_target="tpu_custom_call", output_to_operand_aliasing={{0}: (0, {})} | custom-call | flops 268435456 | bytes 2097152 | tf_op jit(solution)/shard_map/pallas_call | solution.py:256
  37.6 0.0 collective-permute-done.4.cross
  37.6 3.6 %collective-permute-done.3.same = bf16[2064,128]{1,0:T(8,128)(2,1)S(1)} collective-permute-done((bf16[2064,128]{1,0:T(8,128)(2,1)S(1)}, bf16[2064,128]{1,0:T(8,128)(2,1)S(1)}, u32[]{:S(2)}, u32[]{:S(2)}) %collective-permute-start.3) | collective-permute-done | bytes 528416 | tf_op jit(solution)/shard_map/ppermute | solution.py:344
  41.1 0.6 shard_map.53
  41.7 0.0 collective-permute-done.5.refs_0_
  41.7 0.0 collective-permute-done.7.refs_1_
  41.7 0.4 shard_map.54
  42.1 18.5 %all_to_all.11 = f32[128,1,128]{2,1,0:T(1,128)S(1)} all-to-all(f32[128,1,128]{2,1,0:T(1,128)S(1)} %bitcast.6), channel_id=1, replica_groups=mesh['vocab_0'=4,'vocab_1'=4,'vocab_2'=4,'dp'=2] {'vocab_0','vocab_1','v..., dimensions={0} | all-to-all | bytes 131072 | tf_op jit(solution)/shard_map/all_to_all | solution.py:381
  60.6 2.3 %clipped_update.1 = (bf16[1024,2048]{1,0:T(8,128)(2,1)}, f32[1]{0:T(128)}) custom-call(f32[1024,2048]{1,0:T(8,128)S(1)} %get-tuple-element.29.grad_in, bf16[16,1024,128]{2,1,0:T(8,128)(2,1)S(1)} %get-tuple-element.30.table_in, f32[128,128]{1,0:T(8,128)S(1)} %bitcast.5), custom_call_target="tpu_custom_call" | custom-call | tf_op jit(solution)/shard_map/clipped_update/pallas_call | solution.py:297
Async XLA Ops:
  3.2 24.3 %collective-permute-start = (bf16[1040,2048]{1,0:T(8,128)(2,1)S(1)}, bf16[1040,2048]{1,0:T(8,128)(2,1)S(1)}, u32[]{:S(2)}, u32[]{:S(2)}) collective-permute-start(bf16[1040,2048]{1,0:T(8,128)(2,1)S(1)} %get-tuple-element.17), channel_id=1, source_target_pairs={{0,1},{1,0},{2,3},{3,2},{4,5},{5,4},{6,7},{7,6},{8,9},{9,8},{10,11... | collective-permute-start | bytes 12779528 | tf_op jit(solution)/shard_map/ppermute | solution.py:344
  4.7 21.1 %collective-permute-start.2 = (bf16[2064,128]{1,0:T(8,128)(2,1)S(1)}, bf16[2064,128]{1,0:T(8,128)(2,1)S(1)}, u32[]{:S(2)}, u32[]{:S(2)}) collective-permute-start(bf16[2064,128]{1,0:T(8,128)(2,1)S(1)} %get-tuple-element.21), channel_id=1, source_target_pairs={{0,3},{1,2},{2,5},{3,4},{4,7},{5,6},{6,9},{7,8},{8,11},{9,10},{10,... | collective-permute-start | bytes 1585160 | tf_op jit(solution)/shard_map/ppermute | solution.py:344
  7.7 8.8 %collective-permute-start.6 = (bf16[640,128]{1,0:T(8,128)(2,1)S(1)}, bf16[640,128]{1,0:T(8,128)(2,1)S(1)}, u32[]{:S(2)}, u32[]{:S(2)}) collective-permute-start(bf16[640,128]{1,0:T(8,128)(2,1)S(1)} %get-tuple-element.28), channel_id=1, source_target_pairs={{0,15},{1,38},{32,47},{33,70},{64,79},{65,102},{96,111},{97,6}} | collective-permute-start | bytes 491528 | tf_op jit(solution)/shard_map/ppermute | solution.py:344
  12.9 28.8 %collective-permute-start.5 = (bf16[640,128]{1,0:T(8,128)(2,1)S(1)}, bf16[640,128]{1,0:T(8,128)(2,1)S(1)}, u32[]{:S(2)}, u32[]{:S(2)}) collective-permute-start(bf16[640,128]{1,0:T(8,128)(2,1)S(1)} %get-tuple-element.28), channel_id=1, source_target_pairs={{2,1},{3,0},{4,3},{5,2},{6,5},{7,4},{8,7},{9,6},{10,9},{11,8},{12,... | collective-permute-start | bytes 491528 | tf_op jit(solution)/shard_map/ppermute | solution.py:344
  14.2 22.6 %collective-permute-start.1 = (bf16[2064,128]{1,0:T(8,128)(2,1)S(1)}, bf16[2064,128]{1,0:T(8,128)(2,1)S(1)}, u32[]{:S(2)}, u32[]{:S(2)}) collective-permute-start(bf16[2064,128]{1,0:T(8,128)(2,1)S(1)} %get-tuple-element.20), channel_id=1, source_target_pairs={{0,2},{1,3},{2,4},{3,5},{4,6},{5,7},{6,8},{7,9},{8,10},{9,11},{10,... | collective-permute-start | bytes 1585160 | tf_op jit(solution)/shard_map/ppermute | solution.py:344
  16.5 21.0 %collective-permute-start.4 = (bf16[1424,128]{1,0:T(8,128)(2,1)S(1)}, bf16[1424,128]{1,0:T(8,128)(2,1)S(1)}, u32[]{:S(2)}, u32[]{:S(2)}) collective-permute-start(bf16[1424,128]{1,0:T(8,128)(2,1)S(1)} %get-tuple-element.25), channel_id=1, source_target_pairs={{0,127},{1,126},{2,1},{3,0},{4,3},{5,2},{6,5},{7,4},{8,7},{9,6},{1... | collective-permute-start | bytes 1093640 | tf_op jit(solution)/shard_map/ppermute | solution.py:344
  25.8 15.4 %collective-permute-start.3 = (bf16[2064,128]{1,0:T(8,128)(2,1)S(1)}, bf16[2064,128]{1,0:T(8,128)(2,1)S(1)}, u32[]{:S(2)}, u32[]{:S(2)}) collective-permute-start(bf16[2064,128]{1,0:T(8,128)(2,1)S(1)} %get-tuple-element.24), channel_id=1, source_target_pairs={{0,126},{1,127},{2,0},{3,1},{4,2},{5,3},{6,4},{7,5},{8,6},{9,7},{1... | collective-permute-start | bytes 1585160 | tf_op jit(solution)/shard_map/ppermute | solution.py:344
  27.5 14.2 %collective-permute-start.7 = (bf16[640,128]{1,0:T(8,128)(2,1)S(1)}, bf16[640,128]{1,0:T(8,128)(2,1)S(1)}, u32[]{:S(2)}, u32[]{:S(2)}) collective-permute-start(bf16[640,128]{1,0:T(8,128)(2,1)S(1)} %collective-permute-done.6), channel_id=1, source_target_pairs={{15,127},{38,126},{47,31},{70,30},{79,63},{102,62},{111,95},{6,94}} | collective-permute-start | bytes 491528 | tf_op jit(solution)/shard_map/ppermute | solution.py:344

commit v4 on v3

--- a/solution.py
+++ b/solution.py
@@ -350,21 +350,24 @@
     tiles = width // replicas // LANES
     kept = tiles - 5
     shape = (rows_dev, vocab_rows)
-    plus_same, minus_same, minus_rest = pack(
+    plus_same, minus_same = pack(
         rows,
         token_ids,
         *shape,
         (
             (last, False, 0, tiles, True),
             (0, False, 0, tiles, True),
-            (0, True, kept, tiles - kept, False),
         ),
         False,
     )
     plus_same = sent(plus_same, 1, False)
     minus_same = sent(minus_same, -1, False)
-    plus_cross, minus_cross, far = pack(
-        rows, token_ids, *shape, ((last, True, 0, tiles, True), (0, True, 0, kept, True)), True
+    plus_cross, minus_cross, minus_rest, far = pack(
+        rows,
+        token_ids,
+        *shape,
+        ((last, True, 0, tiles, True), (0, True, 0, kept, True), (0, True, kept, tiles - kept, False)),
+        True,
     )
     far = sent(far, 0, True)
     minus_cross = sent(minus_cross, -1, True)

time: 63.3 us -> 63.3 us (level)
  no operation moved by 1% of the time
where the time goes in v4:
time: 63.3 us; the launch traced here: 63 us
  starting transfers between devices  19.5 us (31%)
  blocking collectives  18.5 us (29%)
  Pallas kernels  15.1 us (24%)
  waiting for transfers between devices  9.16 us (14%)
  between operations  0.71 us (1%)
    ppermute x8, starting transfers between devices, moved(): return lax.ppermute(piece, VOCAB_DP, pairs)  19.5 us
    all_to_all x1, blocking collectives, body(): partials = lax.all_to_all(spread, VOCAB_DP, 0, 0, tiled=True)  18.5 us
    ppermute x8, waiting for transfers between devices, moved(): return lax.ppermute(piece, VOCAB_DP, pairs)  9.16 us
    pallas_call x1, Pallas kernels, local_gradient(): pl.pallas_call(kernel, out_shape=[pltpu.VMEM((rows_dev, half), jnp.float3...  7.18 us
    pallas_call x2, Pallas kernels, pack(): pl.pallas_call(kernel, out_shape=shapes, in_specs=[any_spec(), any_spec()...  3.88 us
    pallas_call x1, Pallas kernels, clipped_update(): pl.pallas_call(kernel, out_shape=[jax.ShapeDtypeStruct((rows_dev, half),...  2.34 us
    pallas_call x3, Pallas kernels, edge_gradient(): pl.pallas_call(kernel, out_shape=[pltpu.VMEM(grad.shape, jnp.float32), pl...  1.69 us
  transfers between devices with their start and end apart: 8, of which 3 were waited for; matrix products, arithmetic and copies ran while one was open for 0% of the time, Pallas kernels for 15%

profile of v4, /device:TPU:1, one launch (start us, length us, event | category | flops | bytes accessed | tf_op | source)
XLA Modules:
  0.0 63.0 jit_solution(7018328238294832389)
XLA Ops:
  0.6 2.7 %shard_map.50 = (bf16[2064,128]{1,0:T(8,128)(2,1)S(1)}, bf16[1424,128]{1,0:T(8,128)(2,1)S(1)}, bf16[640,128]{1,0:T(8,128)(2,1)S(1)}, bf16[1040,2048]{1,0:T(8,128)(2,1)S(1)}) custom-call(bf16[1024,4096]{1,0:T(8,128)(2,1)} %bitcast.7, s32[1,1024]{1,0:T(1,128)} %ids_in.5), custom_call_target="tpu_custom_call" | custom-call | tf_op jit(solution)/shard_map/pallas_call | solution.py:107
  3.3 1.5 %collective-permute-start = (bf16[1040,2048]{1,0:T(8,128)(2,1)S(1)}, bf16[1040,2048]{1,0:T(8,128)(2,1)S(1)}, u32[]{:S(2)}, u32[]{:S(2)}) collective-permute-start(bf16[1040,2048]{1,0:T(8,128)(2,1)S(1)} %get-tuple-element.17), channel_id=1, source_target_pairs={{0,1},{1,0},{2,3},{3,2},{4,5},{5,4},{6,7},{7,6},{8,9},{9,8},{10,11... | collective-permute-start | bytes 12779528 | tf_op jit(solution)/shard_map/ppermute | solution.py:344
  4.8 1.7 %collective-permute-start.2 = (bf16[2064,128]{1,0:T(8,128)(2,1)S(1)}, bf16[2064,128]{1,0:T(8,128)(2,1)S(1)}, u32[]{:S(2)}, u32[]{:S(2)}) collective-permute-start(bf16[2064,128]{1,0:T(8,128)(2,1)S(1)} %get-tuple-element.21), channel_id=1, source_target_pairs={{0,3},{1,2},{2,5},{3,4},{4,7},{5,6},{6,9},{7,8},{8,11},{9,10},{10,... | collective-permute-start | bytes 1585160 | tf_op jit(solution)/shard_map/ppermute | solution.py:344
  6.5 5.2 %collective-permute-start.6 = (bf16[640,128]{1,0:T(8,128)(2,1)S(1)}, bf16[640,128]{1,0:T(8,128)(2,1)S(1)}, u32[]{:S(2)}, u32[]{:S(2)}) collective-permute-start(bf16[640,128]{1,0:T(8,128)(2,1)S(1)} %get-tuple-element.28), channel_id=1, source_target_pairs={{0,15},{1,38},{32,47},{33,70},{64,79},{65,102},{96,111},{97,6}} | collective-permute-start | bytes 491528 | tf_op jit(solution)/shard_map/ppermute | solution.py:344
  11.7 1.3 %collective-permute-start.5 = (bf16[640,128]{1,0:T(8,128)(2,1)S(1)}, bf16[640,128]{1,0:T(8,128)(2,1)S(1)}, u32[]{:S(2)}, u32[]{:S(2)}) collective-permute-start(bf16[640,128]{1,0:T(8,128)(2,1)S(1)} %get-tuple-element.28), channel_id=1, source_target_pairs={{2,1},{3,0},{4,3},{5,2},{6,5},{7,4},{8,7},{9,6},{10,9},{11,8},{12,... | collective-permute-start | bytes 491528 | tf_op jit(solution)/shard_map/ppermute | solution.py:344
  13.0 1.2 %shard_map.51 = (bf16[2064,128]{1,0:T(8,128)(2,1)S(1)}, bf16[2064,128]{1,0:T(8,128)(2,1)S(1)}) custom-call(bf16[1024,4096]{1,0:T(8,128)(2,1)} %bitcast.8, s32[1,1024]{1,0:T(1,128)} %ids_in.5), custom_call_target="tpu_custom_call" | custom-call | tf_op jit(solution)/shard_map/pallas_call | solution.py:107
  14.2 2.3 %collective-permute-start.1 = (bf16[2064,128]{1,0:T(8,128)(2,1)S(1)}, bf16[2064,128]{1,0:T(8,128)(2,1)S(1)}, u32[]{:S(2)}, u32[]{:S(2)}) collective-permute-start(bf16[2064,128]{1,0:T(8,128)(2,1)S(1)} %get-tuple-element.20), channel_id=1, source_target_pairs={{0,2},{1,3},{2,4},{3,5},{4,6},{5,7},{6,8},{7,9},{8,10},{9,11},{10,... | collective-permute-start | bytes 1585160 | tf_op jit(solution)/shard_map/ppermute | solution.py:344
  16.5 0.0 collective-permute-done.6
  16.5 5.1 %collective-permute-start.4 = (bf16[1424,128]{1,0:T(8,128)(2,1)S(1)}, bf16[1424,128]{1,0:T(8,128)(2,1)S(1)}, u32[]{:S(2)}, u32[]{:S(2)}) collective-permute-start(bf16[1424,128]{1,0:T(8,128)(2,1)S(1)} %get-tuple-element.25), channel_id=1, source_target_pairs={{0,127},{1,126},{2,1},{3,0},{4,3},{5,2},{6,5},{7,4},{8,7},{9,6},{1... | collective-permute-start | bytes 1093640 | tf_op jit(solution)/shard_map/ppermute | solution.py:344
  21.6 4.2 %collective-permute-done.2.cross = bf16[2064,128]{1,0:T(8,128)(2,1)S(1)} collective-permute-done((bf16[2064,128]{1,0:T(8,128)(2,1)S(1)}, bf16[2064,128]{1,0:T(8,128)(2,1)S(1)}, u32[]{:S(2)}, u32[]{:S(2)}) %collective-permute-start.2) | collective-permute-done | bytes 528416 | tf_op jit(solution)/shard_map/ppermute | solution.py:344
  25.8 1.8 %collective-permute-start.3 = (bf16[2064,128]{1,0:T(8,128)(2,1)S(1)}, bf16[2064,128]{1,0:T(8,128)(2,1)S(1)}, u32[]{:S(2)}, u32[]{:S(2)}) collective-permute-start(bf16[2064,128]{1,0:T(8,128)(2,1)S(1)} %get-tuple-element.24), channel_id=1, source_target_pairs={{0,126},{1,127},{2,0},{3,1},{4,2},{5,3},{6,4},{7,5},{8,6},{9,7},{1... | collective-permute-start | bytes 1585160 | tf_op jit(solution)/shard_map/ppermute | solution.py:344
  27.6 0.0 collective-permute-done.far_rows
  27.6 0.7 %collective-permute-start.7 = (bf16[640,128]{1,0:T(8,128)(2,1)S(1)}, bf16[640,128]{1,0:T(8,128)(2,1)S(1)}, u32[]{:S(2)}, u32[]{:S(2)}) collective-permute-start(bf16[640,128]{1,0:T(8,128)(2,1)S(1)} %collective-permute-done.6), channel_id=1, source_target_pairs={{15,127},{38,126},{47,31},{70,30},{79,63},{102,62},{111,95},{6,94}} | collective-permute-start | bytes 491528 | tf_op jit(solution)/shard_map/ppermute | solution.py:344
  28.2 7.2 %local_gradient.1 = (f32[1024,2048]{1,0:T(8,128)S(1)}, bf16[16,1024,128]{2,1,0:T(8,128)(2,1)S(1)}, f32[1,128]{1,0:T(1,128)S(1)}) custom-call(bf16[1024,4096]{1,0:T(8,128)(2,1)} %bitcast.9, bf16[1040,2048]{1,0:T(8,128)(2,1)S(1)} %collective-permute-done.far_rows, s32[1,1024]{1,0:T(1,128)} %ids_in.5, bf16[1024,4096]{1,0:T(8,128)(2,1)} %table.1), custom_call_target="tpu_custom_call" | custom-call | flops 8589934592 | bytes 8388608 | tf_op jit(solution)/shard_map/local_gradient/pallas_call | solution.py:188
  35.4 1.5 %collective-permute-done.1.same = bf16[2064,128]{1,0:T(8,128)(2,1)S(1)} collective-permute-done((bf16[2064,128]{1,0:T(8,128)(2,1)S(1)}, bf16[2064,128]{1,0:T(8,128)(2,1)S(1)}, u32[]{:S(2)}, u32[]{:S(2)}) %collective-permute-start.1) | collective-permute-done | bytes 528416 | tf_op jit(solution)/shard_map/ppermute | solution.py:344
  36.9 0.7 %shard_map.52 = (f32[1024,2048]{1,0:T(8,128)S(1)}, f32[1,128]{1,0:T(1,128)S(1)}) custom-call(f32[1024,2048]{1,0:T(8,128)S(1)} %get-tuple-element.18.grad_in, f32[1,128]{1,0:T(1,128)S(1)} %get-tuple-element.19.squares_in, bf16[2064,128]{1,0:T(8,128)(2,1)S(1)} %collective-permute-done.1.same, ...), custom_call_target="tpu_custom_call", output_to_operand_aliasing={{0}: (0, {})} | custom-call | flops 268435456 | bytes 2097152 | tf_op jit(solution)/shard_map/pallas_call | solution.py:256
  37.6 0.0 collective-permute-done.4.cross
  37.6 3.5 %collective-permute-done.3.same = bf16[2064,128]{1,0:T(8,128)(2,1)S(1)} collective-permute-done((bf16[2064,128]{1,0:T(8,128)(2,1)S(1)}, bf16[2064,128]{1,0:T(8,128)(2,1)S(1)}, u32[]{:S(2)}, u32[]{:S(2)}) %collective-permute-start.3) | collective-permute-done | bytes 528416 | tf_op jit(solution)/shard_map/ppermute | solution.py:344
  41.1 0.6 shard_map.53
  41.7 0.0 collective-permute-done.5.refs_0_
  41.7 0.0 collective-permute-done.7.refs_1_
  41.7 0.4 shard_map.54
  42.1 18.5 %all_to_all.11 = f32[128,1,128]{2,1,0:T(1,128)S(1)} all-to-all(f32[128,1,128]{2,1,0:T(1,128)S(1)} %bitcast.6), channel_id=1, replica_groups=mesh['vocab_0'=4,'vocab_1'=4,'vocab_2'=4,'dp'=2] {'vocab_0','vocab_1','v..., dimensions={0} | all-to-all | bytes 131072 | tf_op jit(solution)/shard_map/all_to_all | solution.py:384
  60.6 2.3 %clipped_update.1 = (bf16[1024,2048]{1,0:T(8,128)(2,1)}, f32[1]{0:T(128)}) custom-call(f32[1024,2048]{1,0:T(8,128)S(1)} %get-tuple-element.29.grad_in, bf16[16,1024,128]{2,1,0:T(8,128)(2,1)S(1)} %get-tuple-element.30.table_in, f32[128,128]{1,0:T(8,128)S(1)} %bitcast.5), custom_call_target="tpu_custom_call" | custom-call | tf_op jit(solution)/shard_map/clipped_update/pallas_call | solution.py:297
Async XLA Ops:
  3.3 24.3 %collective-permute-start = (bf16[1040,2048]{1,0:T(8,128)(2,1)S(1)}, bf16[1040,2048]{1,0:T(8,128)(2,1)S(1)}, u32[]{:S(2)}, u32[]{:S(2)}) collective-permute-start(bf16[1040,2048]{1,0:T(8,128)(2,1)S(1)} %get-tuple-element.17), channel_id=1, source_target_pairs={{0,1},{1,0},{2,3},{3,2},{4,5},{5,4},{6,7},{7,6},{8,9},{9,8},{10,11... | collective-permute-start | bytes 12779528 | tf_op jit(solution)/shard_map/ppermute | solution.py:344
  4.8 21.1 %collective-permute-start.2 = (bf16[2064,128]{1,0:T(8,128)(2,1)S(1)}, bf16[2064,128]{1,0:T(8,128)(2,1)S(1)}, u32[]{:S(2)}, u32[]{:S(2)}) collective-permute-start(bf16[2064,128]{1,0:T(8,128)(2,1)S(1)} %get-tuple-element.21), channel_id=1, source_target_pairs={{0,3},{1,2},{2,5},{3,4},{4,7},{5,6},{6,9},{7,8},{8,11},{9,10},{10,... | collective-permute-start | bytes 1585160 | tf_op jit(solution)/shard_map/ppermute | solution.py:344
  6.5 10.0 %collective-permute-start.6 = (bf16[640,128]{1,0:T(8,128)(2,1)S(1)}, bf16[640,128]{1,0:T(8,128)(2,1)S(1)}, u32[]{:S(2)}, u32[]{:S(2)}) collective-permute-start(bf16[640,128]{1,0:T(8,128)(2,1)S(1)} %get-tuple-element.28), channel_id=1, source_target_pairs={{0,15},{1,38},{32,47},{33,70},{64,79},{65,102},{96,111},{97,6}} | collective-permute-start | bytes 491528 | tf_op jit(solution)/shard_map/ppermute | solution.py:344
  11.7 30.0 %collective-permute-start.5 = (bf16[640,128]{1,0:T(8,128)(2,1)S(1)}, bf16[640,128]{1,0:T(8,128)(2,1)S(1)}, u32[]{:S(2)}, u32[]{:S(2)}) collective-permute-start(bf16[640,128]{1,0:T(8,128)(2,1)S(1)} %get-tuple-element.28), channel_id=1, source_target_pairs={{2,1},{3,0},{4,3},{5,2},{6,5},{7,4},{8,7},{9,6},{10,9},{11,8},{12,... | collective-permute-start | bytes 491528 | tf_op jit(solution)/shard_map/ppermute | solution.py:344
  14.2 22.7 %collective-permute-start.1 = (bf16[2064,128]{1,0:T(8,128)(2,1)S(1)}, bf16[2064,128]{1,0:T(8,128)(2,1)S(1)}, u32[]{:S(2)}, u32[]{:S(2)}) collective-permute-start(bf16[2064,128]{1,0:T(8,128)(2,1)S(1)} %get-tuple-element.20), channel_id=1, source_target_pairs={{0,2},{1,3},{2,4},{3,5},{4,6},{5,7},{6,8},{7,9},{8,10},{9,11},{10,... | collective-permute-start | bytes 1585160 | tf_op jit(solution)/shard_map/ppermute | solution.py:344
  16.5 21.1 %collective-permute-start.4 = (bf16[1424,128]{1,0:T(8,128)(2,1)S(1)}, bf16[1424,128]{1,0:T(8,128)(2,1)S(1)}, u32[]{:S(2)}, u32[]{:S(2)}) collective-permute-start(bf16[1424,128]{1,0:T(8,128)(2,1)S(1)} %get-tuple-element.25), channel_id=1, source_target_pairs={{0,127},{1,126},{2,1},{3,0},{4,3},{5,2},{6,5},{7,4},{8,7},{9,6},{1... | collective-permute-start | bytes 1093640 | tf_op jit(solution)/shard_map/ppermute | solution.py:344
  25.8 15.3 %collective-permute-start.3 = (bf16[2064,128]{1,0:T(8,128)(2,1)S(1)}, bf16[2064,128]{1,0:T(8,128)(2,1)S(1)}, u32[]{:S(2)}, u32[]{:S(2)}) collective-permute-start(bf16[2064,128]{1,0:T(8,128)(2,1)S(1)} %get-tuple-element.24), channel_id=1, source_target_pairs={{0,126},{1,127},{2,0},{3,1},{4,2},{5,3},{6,4},{7,5},{8,6},{9,7},{1... | collective-permute-start | bytes 1585160 | tf_op jit(solution)/shard_map/ppermute | solution.py:344
  27.6 14.1 %collective-permute-start.7 = (bf16[640,128]{1,0:T(8,128)(2,1)S(1)}, bf16[640,128]{1,0:T(8,128)(2,1)S(1)}, u32[]{:S(2)}, u32[]{:S(2)}) collective-permute-start(bf16[640,128]{1,0:T(8,128)(2,1)S(1)} %collective-permute-done.6), channel_id=1, source_target_pairs={{15,127},{38,126},{47,31},{70,30},{79,63},{102,62},{111,95},{6,94}} | collective-permute-start | bytes 491528 | tf_op jit(solution)/shard_map/ppermute | solution.py:344
